TPU v7x, 32 devices: a whole 2x2x4 slice. The times are simulated.
32 devices in a mesh: groups: 2 (over y), seq: 4 (over z), head: 4 (over x, core).
Axes of the slice: x: 2, y: 2, z: 4, core: 2. Of those that a mesh axis runs over, the one named last changes fastest.
Arguments:
- tile_tokens: bfloat16 [16, 256, 1536], P(('groups', 'seq')), parts along dimension 0, may hold values from -6 to 6
- tile_gain: float32 [1536], replicated, may hold values from 0.1 to 1.9
- w_gate_up: bfloat16 [2, 1536, 4096], P(None, 'seq', 'head'), may hold values from -0.15625 to 0.15625
- w_down: bfloat16 [4096, 1536], P('head', 'seq'), may hold values from -0.09375 to 0.09375
- layer_scale: float32 [1536], replicated, may hold values from 1 to 8
- fc_gain: float32 [1536], replicated, may hold values from 0.1 to 1.9
- w_embed: bfloat16 [1536, 768], P(None, 'head'), may hold values from -0.15625 to 0.15625
- embed_bias: float32 [768], P('head'), may hold values from -3 to 3
- pre_emb: bfloat16 [2032, 768], P(('groups', 'seq'), 'head'), parts along dimension 0, may hold values from -6 to 6
- tile_order: int32 [2048], P('groups'), parts along dimension 0, may hold values from 0 to 1023, as said below
- valid_count: int32 [2], P('groups'), parts along dimension 0, may hold values from 256 to 1024
- slide_gain: float32 [768], replicated, may hold values from 0.1 to 1.9
- w_qkv: bfloat16 [3, 768, 768], P(None, None, 'head'), may hold values from -1.25 to 1.25
- sub_gain: float32 [768], P('head'), may hold values from 0.1 to 1.9
- w_out: bfloat16 [768, 768], P('head'), may hold values from -0.21875 to 0.21875
Outputs:
- mixed: float32 [2048, 768], P(('groups', 'seq'), 'head'), parts along dimension 0
There are 2 independent parts, one for each index of `groups`. A program takes and returns all parts, laid end to end along the dimension named above; an argument that names none is the same for every part. Nothing has to cross between parts.
Inputs may be any that keep to these rules, and one draw needn't show every extreme that they name: `tile_order`: A permutation of 0 to 1023. For every block of 256 positions (d * 256 to (d + 1) * 256 - 1) and every block of 256 stored rows, exactly 64 positions of the first take rows of the second.
All inputs are finite; a program needn't handle non-finite values.
Results may differ from a plain program's by a relative error of at most 0.0046.
Values may be sent and summed in bfloat16 or wider, within the bound.
A program may use at most 64 MiB of HBM per device.

v0:
```python
import functools
import math

import jax
import jax.numpy as jnp
from jax import lax
from jax.experimental import pallas as pl
from jax.experimental.pallas import tpu as pltpu
from jax.sharding import PartitionSpec as P

DS = 768
HEAD_DIM = 48
SPAN0 = 1024
SPAN1 = 4096
DILATION_SECOND = 4
DILATION_THIRD = 16


layer_eps = 1e-05
masked_score = -1e30


def from_partner(value, axis, bit):
    mask = 2**bit
    pairs = [(source, source ^ mask) for source in range(lax.axis_size(axis))]
    return lax.ppermute(value, axis, pairs)


def normalize(values, gain):
    centered = values - jnp.mean(values, axis=-1, keepdims=True)
    variance = jnp.mean(centered * centered, axis=-1, keepdims=True)
    return centered * lax.rsqrt(variance + layer_eps) * gain


def select_rows(stacked, dilation, offsets):
    group_count, row_count, row_width = stacked.shape
    head_count = offsets.shape[0]
    arranged = stacked.reshape(
        group_count, row_count // dilation, dilation, head_count, row_width // head_count
    )
    choose = jnp.arange(dilation, dtype=jnp.int32)[:, None] == offsets[None, :]
    chosen = jnp.sum(
        jnp.where(choose[None, None, :, :, None], arranged, jnp.zeros((), stacked.dtype)), axis=2
    )
    return chosen.reshape(group_count, row_count // dilation, row_width)


def scatter_rows(attended, log_mass, dilation, offsets):
    query_count, head_count, head_size = attended.shape
    choose = jnp.arange(dilation, dtype=jnp.int32)[:, None] == offsets[None, :]
    spread_out = jnp.where(choose[None, :, :, None], attended[:, None, :, :], 0.0).reshape(
        query_count * dilation, head_count, head_size
    )
    spread_mass = jnp.where(choose[None, :, :], log_mass[:, None, :], masked_score).reshape(
        query_count * dilation, head_count
    )
    selected = jnp.broadcast_to(choose[None, :, :], (query_count, dilation, head_count)).reshape(
        query_count * dilation, head_count
    )
    return (spread_out, spread_mass, selected)


def attend(query_rows, key_rows, value_rows, positions, valid_limit, head_count):
    head_size = query_rows.shape[1] // head_count
    query_heads = query_rows.reshape(query_rows.shape[0], head_count, head_size)
    key_heads = key_rows.reshape(key_rows.shape[0], head_count, head_size)
    value_heads = value_rows.reshape(value_rows.shape[0], head_count, head_size)
    scores = jnp.einsum(
        "qhe,khe->hqk", query_heads, key_heads, preferred_element_type=jnp.float32
    ) / math.sqrt(head_size)
    scores = jnp.where((positions < valid_limit)[:, None, :], scores, masked_score)
    highest = jnp.max(scores, axis=-1, keepdims=True)
    exponent = jnp.exp(scores - highest)
    mass_sum = jnp.sum(exponent, axis=-1, keepdims=True)
    weights = (exponent / mass_sum).astype(jnp.bfloat16)
    attended = jnp.einsum("hqk,khe->qhe", weights, value_heads, preferred_element_type=jnp.float32)
    return (attended, (highest[..., 0] + jnp.log(mass_sum[..., 0])).T)


def general_body(
    tile_tokens,
    tile_gain,
    w_gate_up,
    w_down,
    layer_scale,
    fc_gain,
    w_embed,
    embed_bias,
    pre_emb,
    tile_order,
    valid_count,
    slide_gain,
    w_qkv,
    sub_gain,
    w_out,
):
    new_count, patch_count, tile_width = tile_tokens.shape
    token_rows = tile_tokens.reshape(new_count * patch_count, tile_width)
    normed = normalize(token_rows.astype(jnp.float32), tile_gain).astype(jnp.bfloat16)
    hidden_width = w_gate_up.shape[2]
    gate_up = jnp.einsum(
        "rk,gkf->grf",
        normed,
        lax.all_gather(w_gate_up, "seq", axis=1, tiled=True),
        preferred_element_type=jnp.float32,
    )
    hidden = (jax.nn.silu(gate_up[0]) * gate_up[1]).astype(jnp.bfloat16)
    pooled_hidden = jnp.mean(
        hidden.reshape(new_count, patch_count, hidden_width), axis=1, dtype=jnp.float32
    )
    everyone = lax.all_gather(pooled_hidden, "seq", axis=0, tiled=True)
    local_part = jnp.dot(everyone, w_down.astype(jnp.float32), precision=lax.Precision.HIGHEST)
    pooled_part = lax.all_to_all(local_part, "seq", split_axis=0, concat_axis=1, tiled=True)
    summed = lax.psum(pooled_part, "head")
    pooled = jnp.mean(tile_tokens, axis=1, dtype=jnp.float32) + layer_scale * summed
    feature = normalize(pooled, fc_gain).astype(jnp.bfloat16)
    new_rows = (jnp.dot(feature, w_embed, preferred_element_type=jnp.float32) + embed_bias).astype(
        jnp.bfloat16
    )
    stored = jnp.concatenate([new_rows, pre_emb], axis=0)
    block_rows = stored.shape[0]
    total_rows = tile_order.shape[0]
    peer_rows = block_rows // lax.axis_size("seq")
    device = lax.axis_index("seq")
    local_index = jnp.arange(block_rows, dtype=jnp.int32)
    inverse = (
        jnp.zeros((total_rows,), jnp.int32)
        .at[tile_order]
        .set(jnp.arange(total_rows, dtype=jnp.int32))
    )
    placed = lax.dynamic_slice_in_dim(inverse, device * block_rows, block_rows)
    target = placed // block_rows
    before = (target[:, None] == target[None, :]) & (placed[None, :] < placed[:, None])
    slot_index = target * peer_rows + jnp.sum(before, axis=1, dtype=jnp.int32)
    routing = (slot_index[None, :] == local_index[:, None]).astype(jnp.bfloat16)
    outgoing = jnp.dot(routing, stored, preferred_element_type=jnp.float32).astype(jnp.bfloat16)
    incoming = lax.all_to_all(outgoing, "seq", split_axis=0, concat_axis=0, tiled=True)
    wanted = lax.dynamic_slice_in_dim(tile_order, device * block_rows, block_rows)
    source = wanted // block_rows
    earlier = (source[:, None] == source[None, :]) & (local_index[None, :] < local_index[:, None])
    arrival = source * peer_rows + jnp.sum(earlier, axis=1, dtype=jnp.int32)
    own_part = jnp.take(incoming, arrival, axis=0)
    sequence = lax.all_gather(own_part, "head", axis=1, tiled=True)
    slide_normed = normalize(sequence.astype(jnp.float32), slide_gain).astype(jnp.bfloat16)
    projected_rows = jnp.einsum(
        "rd,gdc->grc", slide_normed, w_qkv, preferred_element_type=jnp.float32
    ).astype(jnp.bfloat16)
    cols_here = projected_rows.shape[2]
    head_count = cols_here // HEAD_DIM
    head_indices = lax.axis_index("head") * head_count + jnp.arange(head_count, dtype=jnp.int32)
    valid_limit = valid_count[0]
    row_index = device * block_rows + local_index
    near_devices = min(SPAN0, total_rows) // block_rows
    near_rows = projected_rows[1:]
    for bit_index in range(near_devices.bit_length() - 1):
        partner = from_partner(near_rows, "seq", bit_index)
        upper_half = device // (1 << bit_index) % 2 == 1
        near_rows = jnp.where(
            upper_half,
            jnp.concatenate([partner, near_rows], 1),
            jnp.concatenate([near_rows, partner], 1),
        )
    near_start = device // near_devices * near_devices * block_rows
    near_pos = jnp.broadcast_to(
        near_start + jnp.arange(near_rows.shape[1], dtype=jnp.int32),
        (head_count, near_rows.shape[1]),
    )
    near_out, near_mass = attend(
        projected_rows[0], near_rows[0], near_rows[1], near_pos, valid_limit, head_count
    )
    near_sel = jnp.ones((block_rows, head_count), dtype=bool)
    middle_level_offsets = head_indices % DILATION_SECOND
    middle_level = select_rows(projected_rows, DILATION_SECOND, middle_level_offsets)
    middle_devices = min(SPAN1, total_rows) // block_rows
    middle_key_value = middle_level[1:]
    every_row = lax.all_gather(middle_key_value, "seq", axis=1, tiled=True)
    group_rows = middle_devices * middle_key_value.shape[1]
    middle_key_value = lax.dynamic_slice_in_dim(
        every_row, device // middle_devices * group_rows, group_rows, 1
    )
    middle_start = device // middle_devices * middle_devices * block_rows
    middle_pos = (
        middle_start
        + middle_level_offsets[:, None]
        + DILATION_SECOND * jnp.arange(middle_key_value.shape[1], dtype=jnp.int32)[None, :]
    )
    middle_attention, middle_log_sum = attend(
        middle_level[0],
        middle_key_value[0],
        middle_key_value[1],
        middle_pos,
        valid_limit,
        head_count,
    )
    middle_output, middle_level_mass, middle_selected = scatter_rows(
        middle_attention, middle_log_sum, DILATION_SECOND, middle_level_offsets
    )
    distant_offsets = head_indices % DILATION_THIRD
    distant_local_rows = select_rows(projected_rows, DILATION_THIRD, distant_offsets)
    distant_key_value = lax.all_gather(distant_local_rows[1:], "seq", axis=1, tiled=True)
    distant_positions = (
        distant_offsets[:, None]
        + DILATION_THIRD * jnp.arange(distant_key_value.shape[1], dtype=jnp.int32)[None, :]
    )
    distant_attention, distant_log_sum = attend(
        distant_local_rows[0],
        distant_key_value[0],
        distant_key_value[1],
        distant_positions,
        valid_limit,
        head_count,
    )
    distant_output, distant_mass, distant_selected = scatter_rows(
        distant_attention, distant_log_sum, DILATION_THIRD, distant_offsets
    )
    outputs = jnp.stack([near_out, middle_output, distant_output])
    masses = jnp.stack([near_mass, middle_level_mass, distant_mass])
    selects = jnp.stack([near_sel, middle_selected, distant_selected])
    ceiling = jnp.max(masses, axis=0)
    shares = jnp.where(selects, jnp.exp(masses - ceiling), 0.0)
    combined = jnp.sum(shares[..., None] * outputs, axis=0) / jnp.sum(shares, axis=0)[..., None]
    combined = jnp.where((row_index < valid_limit)[:, None, None], combined, 0.0).reshape(
        block_rows, cols_here
    )
    row_total, row_square = lax.psum(
        (jnp.sum(combined, axis=1), jnp.sum(combined * combined, axis=1)), "head"
    )
    mean_value = row_total / DS
    mean_square = row_square / DS
    scaling = lax.rsqrt(mean_square - mean_value * mean_value + layer_eps)
    settled = ((combined - mean_value[:, None]) * scaling[:, None] * sub_gain).astype(jnp.bfloat16)
    partial_rows = jnp.dot(settled, w_out, preferred_element_type=jnp.float32)
    branch_sum = lax.psum_scatter(partial_rows, "head", scatter_dimension=1, tiled=True)
    return own_part.astype(jnp.float32) + branch_sum


MESH = pl.DeviceIdType.MESH
W_CHUNKS = 8
W_CARRY = 4


def remote(src, dst, send_sem, recv_sem, device):
    return pltpu.make_async_remote_copy(
        src_ref=src,
        dst_ref=dst,
        send_sem=send_sem,
        recv_sem=recv_sem,
        device_id=device,
        device_id_type=MESH,
    )


def dot_rows(left, right):
    return lax.dot_general(
        left, right, (((1,), (1,)), ((), ())), preferred_element_type=jnp.float32
    )


def encode_kernel(
    tiles,
    valid_ref,
    tok_hbm,
    gain_ref,
    scale_ref,
    fc_ref,
    w_ref,
    down_hbm,
    embed_hbm,
    pre_ref,
    wcol_ref,
    bias_ref,
    sub_ref,
    order_ref,
    slide_ref,
    qkv_hbm,
    out_ref,
    tok_ref,
    down_ref,
    embed_ref,
    qkv_ref,
    qkv_parts,
    wcol_parts,
    narrow_ref,
    pre_out,
    new_out,
    wcol_out,
    sub_out,
    seq_rows,
    projected,
    fresh_pick,
    fresh_rows,
    own_query,
    mid_out,
    mid_mass,
    far_out,
    far_mass,
    slots,
    local_sem,
    send_tok,
    recv_tok,
    send_mix,
    recv_mix,
    wall,
    normed,
    acc,
    pooled,
    means,
    parts,
    send_w,
    recv_w,
    send_y,
    recv_y,
    send_pre,
    recv_pre,
    send_fan,
    recv_fan,
    send_aux,
    recv_aux,
    send_seq,
    recv_seq,
    send_part,
    recv_part,
    send_new,
    recv_new,
):
    n = lax.axis_size("seq")
    heads = lax.axis_size("head")
    groups = lax.axis_size("groups")
    z = lax.axis_index("seq")
    hd = lax.axis_index("head")
    y = lax.axis_index("groups")
    rows, width = tok_hbm.shape
    patch = rows // tiles
    depth = width // n
    hidden_width = w_ref.shape[2]
    half = W_CHUNKS // 2
    narrow = wcol_ref.shape[0]
    half_width = hidden_width // 2

    def seq_peer(k):
        return lax.rem(z + k, n)

    def seq_source(k):
        return lax.rem(z + n - k, n)

    def head_peer(k):
        return lax.rem(hd + k, heads)

    def head_source(k):
        return lax.rem(hd + heads - k, heads)

    if groups == 2:
        carry, swap = W_CARRY, W_CHUNKS - W_CARRY

        def chunk(side, i):
            return side * (W_CHUNKS - 1) + i * (1 - 2 * side)

    else:
        carry, swap = W_CHUNKS, 0

        def chunk(side, i):
            return i

    loads = [
        pltpu.make_async_copy(source, target, local_sem.at[i])
        for i, (source, target) in enumerate(
            (
                (tok_hbm, tok_ref.at[pl.ds(pl.multiple_of(lax.rem(z, 2) * rows, rows), rows)]),
                (qkv_hbm, qkv_ref),
                (down_hbm, down_ref),
                (embed_hbm, embed_ref),
            )
        )
    ]
    for load in loads:
        load.start()
    barrier = pltpu.get_barrier_semaphore()
    count = 0
    for k in range(n):
        for j in range(heads):
            if k or j:
                pl.semaphore_signal(
                    barrier,
                    inc=1,
                    device_id={"seq": seq_peer(k), "head": head_peer(j)},
                    device_id_type=MESH,
                )
                count += 1
    if groups == 2:
        pl.semaphore_signal(barrier, inc=1, device_id={"groups": 1 - y}, device_id_type=MESH)
        count += 1
    pl.semaphore_wait(barrier, count)

    pending = []

    def start(copy, cond=None):
        if cond is None:
            copy.start()
        else:
            pl.when(cond)(copy.start)
        pending.append((copy, cond))

    part = lax.rem(z, 2)
    partner = z + 1 - 2 * part
    quarter = rows // heads

    def token_rows(member, share):
        return pl.ds(pl.multiple_of(member * rows + share * quarter, quarter), quarter)

    start(
        remote(
            tok_hbm.at[pl.ds(pl.multiple_of(hd * quarter, quarter), quarter)],
            tok_ref.at[token_rows(part, hd)],
            send_tok.at[0],
            recv_tok.at[0],
            {"seq": partner},
        )
    )
    for d in range(1, n):
        for i in range(carry):
            c = chunk(y, i)
            for side in range(2):
                goes = z + d < n if side == 0 else z >= d
                target = lax.min(z + d, n - 1) if side == 0 else lax.max(z - d, 0)
                at = pl.ds(pl.multiple_of(lax.rem(target, 2) * half_width, half_width), half_width)
                start(
                    remote(
                        w_ref.at[c, :, at],
                        wall.at[z, c],
                        send_w.at[side, d - 1, i],
                        recv_w.at[side, d - 1, i],
                        {"seq": target},
                    ),
                    goes,
                )
        if d == 1:
            for k in range(1, n):
                start(
                    remote(
                        pre_ref,
                        pre_out.at[z, hd],
                        send_pre.at[k],
                        recv_pre.at[k],
                        {"seq": seq_peer(k)},
                    )
                )
    narrow_ref[pl.ds(0, 1), :] = bias_ref[...].reshape(1, narrow)
    narrow_ref[pl.ds(1, 1), :] = sub_ref[...].reshape(1, narrow)
    for j in range(heads):
        wcol_parts[j] = wcol_ref[:, j * narrow : (j + 1) * narrow]
    for k in range(1, heads):
        start(
            remote(
                wcol_parts.at[head_peer(k)],
                wcol_out.at[hd],
                send_aux.at[0, k],
                recv_aux.at[0, k],
                {"head": head_peer(k)},
            )
        )
        start(
            remote(
                narrow_ref, sub_out.at[hd], send_aux.at[1, k], recv_aux.at[1, k], {"head": head_peer(k)}
            )
        )
        start(
            remote(
                pre_ref,
                pre_out.at[z, hd],
                send_fan.at[0, k],
                recv_fan.at[0, k],
                {"head": head_peer(k)},
            )
        )
    pre_out[z, hd] = pre_ref[...]
    wcol_out[hd] = wcol_parts[hd]
    sub_out[hd] = narrow_ref[...]

    loads[0].wait()
    block = 64

    def norm_tokens(member, keep_mean):
        for tile in range(tiles):

            def norm_rows(i, total):
                at = pl.ds(
                    pl.multiple_of(member * rows + tile * patch + i * block, block), block
                )
                values = tok_ref[at, :].astype(jnp.float32)
                out = normalize(values, gain_ref[...].reshape(1, width)).astype(jnp.bfloat16)
                for b in range(n):
                    normed[b, at, :] = out[:, b * depth : (b + 1) * depth]
                if keep_mean:
                    total = total + jnp.sum(values, axis=0, keepdims=True)
                return total

            total = lax.fori_loop(
                0, patch // block, norm_rows, jnp.zeros((1, width), jnp.float32)
            )
            if keep_mean:
                means[z, pl.ds(tile, 1), :] = total / patch

    norm_tokens(part, True)
    for k in range(1, n):
        start(
            remote(
                means.at[z], means.at[z], send_seq.at[0, k], recv_seq.at[0, k], {"seq": seq_peer(k)}
            )
        )
    slot = tok_ref.at[token_rows(1 - part, hd)]
    remote(slot, slot, send_tok.at[0], recv_tok.at[0], {"seq": partner}).wait_recv()
    for k in range(1, heads):
        start(remote(slot, slot, send_tok.at[k], recv_tok.at[k], {"head": head_peer(k)}))

    columns = 256

    def multiply(weights, owner, first):
        @pl.loop(0, 2 * (half_width // columns))
        def _(t):
            member = lax.rem(t, 2)
            at = pl.ds(pl.multiple_of(t // 2 * columns, columns), columns)
            span = pl.ds(pl.multiple_of(member * rows, rows), rows)
            for g in range(2):
                if owner is None:
                    place = part * half_width + t // 2 * columns
                    w = weights[
                        pl.ds(g * half, half), :, pl.ds(pl.multiple_of(place, columns), columns)
                    ]
                else:
                    w = weights[owner, pl.ds(g * half, half), :, at]
                w = w.reshape(depth, columns)
                x = normed[z if owner is None else owner, span, :]
                value = jnp.dot(x, w, preferred_element_type=jnp.float32)
                if first:
                    acc[g, span, at] = value
                else:
                    acc[g, span, at] += value

    def owner_of(side, d):
        return lax.max(z - d, 0) if side == 0 else lax.min(z + d, n - 1)

    def valid(side, d):
        return z >= d if side == 0 else z + d < n

    def relay(d):
        for i in range(carry):
            c = chunk(y, i)
            for side in range(2):
                o = owner_of(side, d)
                slot = wall.at[o, c]
                there = valid(side, d)
                arrive = remote(
                    slot,
                    slot,
                    send_w.at[side, d - 1, i],
                    recv_w.at[side, d - 1, i],
                    {"seq": o},
                )
                pl.when(there)(arrive.wait_recv)
                if i < swap:
                    start(
                        remote(
                            slot,
                            slot,
                            send_y.at[side, d - 1, i],
                            recv_y.at[side, d - 1, i],
                            {"groups": 1 - y},
                        ),
                        there,
                    )

    def finish(d):
        for side in range(2):
            o = owner_of(side, d)

            @pl.when(valid(side, d))
            def _():
                for i in range(swap):
                    slot = wall.at[o, chunk(1 - y, i)]
                    remote(
                        slot,
                        slot,
                        send_y.at[side, d - 1, i],
                        recv_y.at[side, d - 1, i],
                        {"groups": 1 - y},
                    ).wait_recv()
                multiply(wall, o, False)

    def fan_out():
        for k in range(1, n):
            slot = pre_out.at[seq_source(k), hd]
            remote(
                slot, slot, send_pre.at[k], recv_pre.at[k], {"seq": seq_peer(k)}
            ).wait_recv()
            for j in range(1, heads):
                start(
                    remote(
                        slot, slot, send_fan.at[k, j], recv_fan.at[k, j], {"head": head_peer(j)}
                    )
                )

    total_rows = order_ref.shape[0]
    cols, stored_rows = pre_ref.shape
    classes = DILATION_THIRD
    class_rows = total_rows // classes
    own_rows = stored_rows // classes

    def row_norm(pieces):
        features = heads * cols
        mean = sum(jnp.sum(p, axis=1, keepdims=True) for p in pieces) / features
        centered = [p - mean for p in pieces]
        variance = sum(jnp.sum(p * p, axis=1, keepdims=True) for p in centered) / features
        scaling = lax.rsqrt(variance + layer_eps)
        return [
            (p * scaling * slide_ref[...].reshape(1, features)[:, j * cols : (j + 1) * cols]).astype(jnp.bfloat16)
            for j, p in enumerate(centered)
        ]

    def project(pieces, g):
        return sum(
            dot_rows(piece, qkv_parts[g, j])
            for j, piece in enumerate(pieces)
        )

    def stored_sequence():
        for k in range(1, heads):
            for b in range(n):
                slot = pre_out.at[seq_source(b), head_source(k)]
                remote(
                    slot, slot, send_fan.at[b, k], recv_fan.at[b, k], {"head": head_peer(k)}
                ).wait_recv()
        loads[1].wait()
        for g in range(3):
            for j in range(heads):
                qkv_parts[g, j] = qkv_ref[g, :, j * cols : (j + 1) * cols]
        step = stored_rows

        @pl.loop(0, total_rows // step)
        def _(t):
            at = pl.ds(pl.multiple_of(t * step, step), step)
            order = order_ref[at, :]
            lane = lax.broadcasted_iota(jnp.int32, (step, 128), 1)
            wanted = jnp.where(
                lane < n * tiles, lane // tiles * stored_rows + lane % tiles, -1
            )
            fresh_pick[at, :] = jnp.where(order == wanted, 1.0, 0.0).astype(jnp.bfloat16)
            index = lax.broadcasted_iota(jnp.int32, (step, stored_rows), 1)
            picks = [
                jnp.where(order == index + b * stored_rows, 1.0, 0.0).astype(jnp.bfloat16)
                for b in range(n)
            ]
            pieces = []
            for j in range(heads):
                piece = sum(
                    dot_rows(picks[b], pre_out[b, j])
                    for b in range(n)
                )
                seq_rows[j, at, :] = piece.astype(jnp.bfloat16)
                pieces.append(piece)
            normal = row_norm(pieces)
            for g in range(3):
                projected[g, at, :] = project(normal, g).astype(jnp.bfloat16)

    relay(1)
    fan_out()
    for k in range(1, heads):
        slot = tok_ref.at[token_rows(1 - part, head_source(k))]
        remote(slot, slot, send_tok.at[k], recv_tok.at[k], {"head": head_peer(k)}).wait_recv()
    norm_tokens(1 - part, False)
    multiply(w_ref, None, True)
    for d in range(2, n):
        if d == n - 1:
            stored_sequence()
        relay(d)
        finish(d - 1)
    if n == 2:
        stored_sequence()
    finish(n - 1)

    for tile in range(2 * tiles):

        @pl.loop(0, half_width // columns)
        def _(t):
            at = pl.ds(pl.multiple_of(t * columns, columns), columns)
            span = pl.ds(tile * patch, patch)
            gate = acc[0, span, at]
            hidden = (gate / (1.0 + jnp.exp(-gate)) * acc[1, span, at]).astype(jnp.bfloat16)
            pooled[z, pl.ds(tile, 1), at] = (
                jnp.sum(hidden.astype(jnp.float32), axis=0, keepdims=True) / patch
            )

    for k in range(1, n):
        start(
            remote(
                pooled.at[z],
                pooled.at[z],
                send_seq.at[1, k],
                recv_seq.at[1, k],
                {"seq": seq_peer(k)},
            )
        )
    for k in range(1, n):
        for which, buffer in ((0, means), (1, pooled)):
            slot = buffer.at[seq_source(k)]
            remote(
                slot, slot, send_seq.at[which, k], recv_seq.at[which, k], {"seq": seq_peer(k)}
            ).wait_recv()
    loads[2].wait()
    loads[3].wait()
    everyone = jnp.concatenate(
        [jnp.concatenate([pooled[b], pooled[b + 1]], axis=1) for b in range(0, n, 2)], axis=0
    )
    high = everyone.astype(jnp.bfloat16)
    rest = everyone - high.astype(jnp.float32)
    middle = rest.astype(jnp.bfloat16)
    low = (rest - middle.astype(jnp.float32)).astype(jnp.bfloat16)
    local_part = jnp.zeros((n * tiles, down_ref.shape[1]), jnp.float32)
    for piece in (low, middle, high):
        local_part += jnp.dot(piece, down_ref[...], preferred_element_type=jnp.float32)
    parts[z, hd] = local_part
    for k in range(n):
        for j in range(heads):
            if k or j:
                start(
                    remote(
                        parts.at[z, hd],
                        parts.at[z, hd],
                        send_part.at[k, j],
                        recv_part.at[k, j],
                        {"seq": seq_peer(k), "head": head_peer(j)},
                    )
                )
    for k in range(n):
        for j in range(heads):
            if k or j:
                slot = parts.at[seq_source(k), head_source(j)]
                remote(
                    slot,
                    slot,
                    send_part.at[k, j],
                    recv_part.at[k, j],
                    {"seq": seq_peer(k), "head": head_peer(j)},
                ).wait_recv()
    summed = jnp.concatenate(
        [sum(parts[b, j] for j in range(heads)) for b in range(n)], axis=1
    )
    average = jnp.concatenate([means[b] for b in range(n)], axis=0)
    feature = normalize(average + scale_ref[...].reshape(1, width) * summed, fc_ref[...].reshape(1, width)).astype(jnp.bfloat16)
    fresh = dot_rows(feature, embed_ref[...]) + narrow_ref[pl.ds(0, 1), :]
    new_out[hd] = fresh
    for k in range(1, heads):
        start(
            remote(
                new_out.at[hd], new_out.at[hd], send_new.at[k], recv_new.at[k], {"head": head_peer(k)}
            )
        )
    for k in range(1, heads):
        peer = {"head": head_peer(k)}
        source = head_source(k)
        for slot, sends, receives in (
            (new_out.at[source], send_new.at[k], recv_new.at[k]),
            (wcol_out.at[source], send_aux.at[0, k], recv_aux.at[0, k]),
            (sub_out.at[source], send_aux.at[1, k], recv_aux.at[1, k]),
        ):
            remote(slot, slot, sends, receives, peer).wait_recv()

    pieces = [new_out[j].astype(jnp.bfloat16).astype(jnp.float32) for j in range(heads)]
    normal = row_norm(pieces)
    fresh_rows[...] = jnp.zeros(fresh_rows.shape, jnp.float32)
    filled = pl.ds(0, n * tiles)
    for g in range(3):
        fresh_rows[g, filled, :] = project(normal, g)
    fresh_rows[3, filled, :] = new_out[hd]
    own_at = pl.ds(pl.multiple_of(z * own_rows, own_rows), own_rows)
    updated = []
    for g in range(3):
        placed = jnp.dot(
            fresh_pick[...],
            fresh_rows[g].astype(jnp.bfloat16),
            preferred_element_type=jnp.float32,
        )
        projected[g] = (projected[g].astype(jnp.float32) + placed).astype(jnp.bfloat16)
    seq_rows[hd] = (
        seq_rows[hd].astype(jnp.float32)
        + jnp.dot(
            fresh_pick[...],
            fresh_rows[3].astype(jnp.bfloat16),
            preferred_element_type=jnp.float32,
        )
    ).astype(jnp.bfloat16)

    def class_part(buffer, lead, c):
        return buffer[lead, pl.ds(pl.multiple_of(c * class_rows, class_rows), class_rows), :]

    for c in range(classes):
        at = pl.ds(
            pl.multiple_of(c * class_rows + z * own_rows, own_rows), own_rows
        )
        own_query[c] = projected[0, at, :]
        out_ref[pl.ds(c * own_rows, own_rows), :] = seq_rows[hd, at, :].astype(jnp.float32)

    limit = valid_ref[0]
    head_count = cols // HEAD_DIM
    lane_head = lax.broadcasted_iota(jnp.int32, (1, cols), 1) // HEAD_DIM
    factor = 1.0 / math.sqrt(HEAD_DIM)

    def weigh(queries, keys, values, positions):
        scores = (
            lax.dot_general(
                queries, keys, (((1,), (1,)), ((), ())), preferred_element_type=jnp.float32
            )
            * factor
        )
        scores = jnp.where(positions < limit, scores, masked_score)
        peak = jnp.max(scores, axis=1, keepdims=True)
        exponent = jnp.exp(scores - peak)
        mass = jnp.sum(exponent, axis=1, keepdims=True)
        weights = (exponent * (1.0 / mass)).astype(jnp.bfloat16)
        return (
            jnp.dot(weights, values, preferred_element_type=jnp.float32),
            peak + jnp.log(mass),
        )

    block_size = classes * own_rows
    row_index = lax.broadcasted_iota(jnp.int32, (block_size, 1), 0)
    row_class = row_index // own_rows
    row_position = z * block_size + row_index % own_rows * classes + row_class
    near_lane = lax.broadcasted_iota(jnp.int32, (1, total_rows), 1)
    near_position = near_lane % class_rows * classes + near_lane // class_rows
    repeat = classes // DILATION_SECOND
    mid_lane = lax.broadcasted_iota(jnp.int32, (1, repeat * class_rows), 1)
    far_lane = lax.broadcasted_iota(jnp.int32, (1, class_rows), 1)
    mid_out[...] = jnp.zeros(mid_out.shape, jnp.float32)
    mid_mass[...] = jnp.zeros(mid_mass.shape, jnp.float32)
    far_out[...] = jnp.zeros(far_out.shape, jnp.float32)
    far_mass[...] = jnp.zeros(far_mass.shape, jnp.float32)
    all_queries = own_query[...].reshape(block_size, cols)
    nothing = jnp.zeros((), jnp.bfloat16)
    combined = jnp.zeros((block_size, cols), jnp.float32)
    for j in range(head_count):
        here = lane_head == j
        mid_offset = lax.rem(hd * head_count + j, DILATION_SECOND)
        far_offset = lax.rem(hd * head_count + j, DILATION_THIRD)
        near, near_log = weigh(
            jnp.where(here, all_queries, nothing), projected[1], projected[2], near_position
        )
        mids = [mid_offset + DILATION_SECOND * t for t in range(repeat)]
        mid, mid_log = weigh(
            jnp.where(here, jnp.concatenate([own_query[c] for c in mids], axis=0), nothing),
            jnp.concatenate([class_part(projected, 1, c) for c in mids], axis=0),
            jnp.concatenate([class_part(projected, 2, c) for c in mids], axis=0),
            mid_lane % class_rows * classes
            + mid_lane // class_rows * DILATION_SECOND
            + mid_offset,
        )
        far, far_log = weigh(
            jnp.where(here, own_query[far_offset], nothing),
            class_part(projected, 1, far_offset),
            class_part(projected, 2, far_offset),
            far_lane * classes + far_offset,
        )
        for t, c in enumerate(mids):
            mid_out[j, c] = mid[t * own_rows : (t + 1) * own_rows]
            mid_mass[j, c] = jnp.broadcast_to(
                mid_log[t * own_rows : (t + 1) * own_rows], (own_rows, 128)
            )
        far_out[j, far_offset] = far
        far_mass[j, far_offset] = jnp.broadcast_to(far_log, (own_rows, 128))
        mid_log = mid_mass[j].reshape(block_size, 128)[:, :1]
        far_log = far_mass[j].reshape(block_size, 128)[:, :1]
        mid_used = row_class % DILATION_SECOND == mid_offset
        far_used = row_class == far_offset
        ceiling = jnp.maximum(near_log, jnp.where(mid_used, mid_log, near_log))
        ceiling = jnp.maximum(ceiling, jnp.where(far_used, far_log, near_log))
        near_share = jnp.exp(near_log - ceiling)
        mid_share = jnp.where(mid_used, jnp.exp(mid_log - ceiling), 0.0)
        far_share = jnp.where(far_used, jnp.exp(far_log - ceiling), 0.0)
        mixture = (
            near_share * near
            + mid_share * mid_out[j].reshape(block_size, cols)
            + far_share * far_out[j].reshape(block_size, cols)
        ) / (near_share + mid_share + far_share)
        combined = jnp.where(here, mixture, combined)
    combined = jnp.where(row_position < limit, combined, 0.0)

    slots[hd] = combined.astype(jnp.bfloat16)
    for k in range(1, heads):
        start(
            remote(
                slots.at[hd], slots.at[hd], send_mix.at[k], recv_mix.at[k], {"head": head_peer(k)}
            )
        )
    for k in range(1, heads):
        slot = slots.at[head_source(k)]
        remote(slot, slot, send_mix.at[k], recv_mix.at[k], {"head": head_peer(k)}).wait_recv()
    pieces = [slots[j].astype(jnp.float32) for j in range(heads)]
    features = heads * cols
    mean = sum(jnp.sum(p, axis=1, keepdims=True) for p in pieces) / features
    square = sum(jnp.sum(p * p, axis=1, keepdims=True) for p in pieces) / features
    scaling = lax.rsqrt(square - mean * mean + layer_eps)
    branch = jnp.zeros(out_ref.shape, jnp.float32)
    for j in range(heads):
        gain = sub_out[j][1:2]
        settled = ((pieces[j] - mean) * scaling * gain).astype(jnp.bfloat16)
        branch += jnp.dot(settled, wcol_out[j], preferred_element_type=jnp.float32)
    out_ref[...] += branch
    for copy, cond in pending:
        if cond is None:
            copy.wait_send()
        else:
            pl.when(cond)(copy.wait_send)


def near_body(
    tile_tokens,
    tile_gain,
    w_gate_up,
    w_down,
    layer_scale,
    fc_gain,
    w_embed,
    embed_bias,
    pre_emb,
    tile_order,
    valid_count,
    slide_gain,
    w_qkv,
    sub_gain,
    w_out,
):
    n = lax.axis_size("seq")
    heads = lax.axis_size("head")
    tiles, patch, width = tile_tokens.shape
    depth, hidden_width = w_gate_up.shape[1:]
    rows = tiles * patch
    cols = w_embed.shape[1]
    head_count = cols // HEAD_DIM
    total_rows = tile_order.shape[0]
    block_rows = total_rows // n
    classes = DILATION_THIRD
    own_rows = block_rows // classes
    by_class = tile_order.reshape(total_rows // classes, classes).T.reshape(total_rows, 1)
    vmem = pl.BlockSpec(memory_space=pltpu.VMEM)
    anywhere = pl.BlockSpec(memory_space=pl.ANY)
    dma = pltpu.SemaphoreType.DMA
    hops = max(n - 1, 1)
    f32, bf16 = jnp.float32, jnp.bfloat16
    out = pl.pallas_call(
        functools.partial(encode_kernel, tiles),
        out_shape=jax.ShapeDtypeStruct((block_rows, cols), f32),
        in_specs=[
            pl.BlockSpec(memory_space=pltpu.SMEM),
            anywhere,
            vmem,
            vmem,
            vmem,
            vmem,
            anywhere,
            anywhere,
            vmem,
            vmem,
            vmem,
            vmem,
            vmem,
            vmem,
            anywhere,
        ],
        out_specs=vmem,
        scratch_shapes=[
            pltpu.VMEM((2 * rows, width), bf16),
            pltpu.VMEM(w_down.shape, bf16),
            pltpu.VMEM((cols, width), bf16),
            pltpu.VMEM((3, cols, heads * cols), bf16),
            pltpu.VMEM((3, heads, cols, cols), bf16),
            pltpu.VMEM((heads, cols, cols), bf16),
            pltpu.VMEM((2, cols), f32),
            pltpu.VMEM((n, heads, cols, block_rows), bf16),
            pltpu.VMEM((heads, n * tiles, cols), f32),
            pltpu.VMEM((heads, cols, cols), bf16),
            pltpu.VMEM((heads, 2, cols), f32),
            pltpu.VMEM((heads, total_rows, cols), bf16),
            pltpu.VMEM((3, total_rows, cols), bf16),
            pltpu.VMEM((total_rows, 128), bf16),
            pltpu.VMEM((4, 128, cols), f32),
            pltpu.VMEM((classes, own_rows, cols), bf16),
            pltpu.VMEM((head_count, classes, own_rows, cols), f32),
            pltpu.VMEM((head_count, classes, own_rows, 128), f32),
            pltpu.VMEM((head_count, classes, own_rows, cols), f32),
            pltpu.VMEM((head_count, classes, own_rows, 128), f32),
            pltpu.VMEM((heads, block_rows, cols), bf16),
            dma((4,)),
            dma((heads,)),
            dma((heads,)),
            dma((heads,)),
            dma((heads,)),
            pltpu.VMEM((n, W_CHUNKS, 2 * depth // W_CHUNKS, hidden_width // 2), bf16),
            pltpu.VMEM((n, 2 * rows, depth), bf16),
            pltpu.VMEM((2, 2 * rows, hidden_width // 2), f32),
            pltpu.VMEM((n, 2 * tiles, hidden_width // 2), f32),
            pltpu.VMEM((n, tiles, width), f32),
            pltpu.VMEM((n, heads, n * tiles, w_down.shape[1]), f32),
            dma((2, hops, W_CHUNKS)),
            dma((2, hops, W_CHUNKS)),
            dma((2, hops, W_CHUNKS)),
            dma((2, hops, W_CHUNKS)),
            dma((n,)),
            dma((n,)),
            dma((n, heads)),
            dma((n, heads)),
            dma((2, heads)),
            dma((2, heads)),
            dma((2, n)),
            dma((2, n)),
            dma((n, heads)),
            dma((n, heads)),
            dma((heads,)),
            dma((heads,)),
        ],
        compiler_params=pltpu.CompilerParams(
            collective_id=0, has_side_effects=True, vmem_limit_bytes=58 * 1024 * 1024
        ),
    )(
        valid_count,
        tile_tokens.reshape(rows, width),
        tile_gain,
        layer_scale,
        fc_gain,
        w_gate_up.reshape(W_CHUNKS, 2 * depth // W_CHUNKS, hidden_width),
        w_down,
        w_embed.T,
        jnp.pad(pre_emb.T, ((0, 0), (tiles, 0))),
        w_out,
        embed_bias,
        sub_gain,
        by_class,
        slide_gain,
        w_qkv.swapaxes(1, 2),
    )
    return out.reshape(classes, own_rows, cols).transpose(1, 0, 2).reshape(block_rows, cols)


def body(*args):
    total_rows = args[9].shape[0]
    if total_rows <= SPAN0 and lax.axis_size("seq") % 2 == 0:
        return near_body(*args)
    return general_body(*args)


def solution(mesh):
    placed = (
        P(("groups", "seq"), None, None),
        P(),
        P(None, "seq", "head"),
        P("head", "seq"),
        P(),
        P(),
        P(None, "head"),
        P("head"),
        P(("groups", "seq"), "head"),
        P("groups"),
        P("groups"),
        P(),
        P(None, None, "head"),
        P("head"),
        P("head", None),
    )
    return jax.shard_map(
        body, mesh=mesh, in_specs=placed, out_specs=P(("groups", "seq"), "head"), check_vma=False
    )
```

profile of v0, /device:TPU:0, one launch (start us, length us, event | category | flops | bytes accessed | tf_op | source)
XLA Modules:
  0.0 107.6 jit_solution(12789251719458788751)
XLA Ops:
  0.7 0.8 reshape.20
  1.4 0.1 copy.17
  1.5 1.6 %pad.4.pre_ref = bf16[192,256]{1,0:T(8,128)(2,1)} pad(bf16[192,254]{1,0:T(8,128)(2,1)} %bitcast.17, bf16[]{:T(256)} %constant.2.clone.1), padding=0_0x2_0 | pad | bytes 195842 | tf_op jit(solution)/shard_map/jit(_pad)/pad | solution.py:1031
  3.1 1.3 %reshape.24.order_ref = s32[1024,1]{1,0:T(8,128)} reshape(s32[16,64]{1,0:T(8,128)S(1)} %copy.17) | data formatting | bytes 8192 | tf_op jit(solution)/shard_map/reshape | solution.py:942
  4.4 101.3 %shard_map.145 = f32[256,192]{1,0:T(8,128)} custom-call(s32[1]{0:T(128)S(6)} %copy.21.valid_ref, bf16[512,1536]{1,0:T(8,128)(2,1)} %bitcast.10, f32[1536]{0:T(1024)} %gain_ref.1, f32[1536]{0:T(1024)} %scale_ref.1, f32[1536]{0:T(1024)} %fc_ref.1, bf16[8,96,1024]{2,1,0:T(8,128)(2,1)} %bitcast.11, bf16[1024,384]{1,0:T(8,128)(2,1)} %down_hbm.1, ...), custom_call_target="tpu_custom_call" | custom-call | tf_op jit(solution)/shard_map/pallas_call | solution.py:948
  105.7 1.1 %copy.19 = f32[16,16,192]{2,0,1:T(8,128)S(1)} copy(f32[16,16,192]{2,1,0:T(8,128)} %bitcast.12) | data formatting | bytes 393216 | tf_op jit(solution)/shard_map/reshape | solution.py:1039
  106.8 0.8 copy.20
where the time goes:
time: 109 us; the launch traced here: 108 us
  Pallas kernels  101 us (93%)
  local copies, waits for them, and re-layouts  5.63 us (5%)
    pallas_call x1, Pallas kernels, near_body(): pl.pallas_call(functools.partial(encode_kernel, tiles), out_shape=jax.Sha...  101 us

commit v1 on v0

--- a/solution.py
+++ b/solution.py
@@ -235,8 +235,7 @@
 
 
 MESH = pl.DeviceIdType.MESH
-W_CHUNKS = 8
-W_CARRY = 4
+LANES = 128
 
 
 def remote(src, dst, send_sem, recv_sem, device):
@@ -263,7 +262,7 @@
     gain_ref,
     scale_ref,
     fc_ref,
-    w_ref,
+    w_hbm,
     down_hbm,
     embed_hbm,
     pre_ref,
@@ -295,53 +294,67 @@
     far_out,
     far_mass,
     slots,
+    normed,
+    wall,
+    acc,
+    pool_mine,
+    pooled,
+    sums,
+    means,
+    parts,
     local_sem,
     send_tok,
     recv_tok,
-    send_mix,
-    recv_mix,
-    wall,
-    normed,
-    acc,
-    pooled,
-    means,
-    parts,
     send_w,
     recv_w,
-    send_y,
-    recv_y,
     send_pre,
     recv_pre,
     send_fan,
     recv_fan,
     send_aux,
     recv_aux,
-    send_seq,
-    recv_seq,
+    send_pool,
+    recv_pool,
+    send_mean,
+    recv_mean,
     send_part,
     recv_part,
     send_new,
     recv_new,
+    send_mix,
+    recv_mix,
 ):
     n = lax.axis_size("seq")
     heads = lax.axis_size("head")
-    groups = lax.axis_size("groups")
     z = lax.axis_index("seq")
     hd = lax.axis_index("head")
     y = lax.axis_index("groups")
     rows, width = tok_hbm.shape
     patch = rows // tiles
-    depth = width // n
-    hidden_width = w_ref.shape[2]
-    half = W_CHUNKS // 2
+    depth, hidden_width = w_hbm.shape[1:]
+    quarter = rows // heads
+    share = hidden_width // 4
+    blocks_k = depth // LANES
+    blocks_c = share // LANES
     narrow = wcol_ref.shape[0]
-    half_width = hidden_width // 2
+
+    part = lax.rem(z, 2)
+    pair = z // 2
+    partner = z + 1 - 2 * part
+    at_end = (z == 0) | (z == n - 1)
+    inside = jnp.logical_not(at_end)
+    inner = n - 1 - z
+    outward = jnp.where(z < 2, 0, n - 1)
+    toward = jnp.where(z < 2, 1, n - 1)
+    across = lax.rem(hd + 2, heads)
+    mate = hd + 1 - 2 * lax.rem(hd, 2)
+    beyond = lax.rem(mate + 2, heads)
 
     def seq_peer(k):
         return lax.rem(z + k, n)
 
-    def seq_source(k):
-        return lax.rem(z + n - k, n)
+    def ahead(k):
+        return lax.rem(z + k * toward, n)
 
     def head_peer(k):
         return lax.rem(hd + k, heads)
@@ -349,31 +362,42 @@
     def head_source(k):
         return lax.rem(hd + heads - k, heads)
 
-    if groups == 2:
-        carry, swap = W_CARRY, W_CHUNKS - W_CARRY
-
-        def chunk(side, i):
-            return side * (W_CHUNKS - 1) + i * (1 - 2 * side)
-
-    else:
-        carry, swap = W_CHUNKS, 0
-
-        def chunk(side, i):
-            return i
-
+    def quarter_rows(index):
+        return pl.ds(pl.multiple_of(index * quarter, quarter), quarter)
+
+    def unit(u):
+        return u // blocks_c, u % blocks_c
+
+    def weight_block(owner, u):
+        r, c = unit(u)
+        place = (lax.rem(owner, 2) * 2 + y) * share + c * LANES
+        return w_hbm.at[
+            :, pl.ds(r * LANES, LANES), pl.ds(pl.multiple_of(place, LANES), LANES)
+        ]
+
+    def wall_block(source, u):
+        r, c = unit(u)
+        return wall.at[r, c, :, pl.ds(pl.multiple_of(source * LANES, LANES), LANES), :]
+
+    units = blocks_k * blocks_c
+    half = quarter // 2
+    first_quarters = (hd, across, mate, beyond)
+    token_loads = [
+        pltpu.make_async_copy(
+            tok_hbm.at[quarter_rows(q)], tok_ref.at[quarter_rows(q)], local_sem.at[i]
+        )
+        for i, q in enumerate(first_quarters)
+    ]
     loads = [
-        pltpu.make_async_copy(source, target, local_sem.at[i])
+        pltpu.make_async_copy(source, target, local_sem.at[4 + i])
         for i, (source, target) in enumerate(
-            (
-                (tok_hbm, tok_ref.at[pl.ds(pl.multiple_of(lax.rem(z, 2) * rows, rows), rows)]),
-                (qkv_hbm, qkv_ref),
-                (down_hbm, down_ref),
-                (embed_hbm, embed_ref),
-            )
+            ((qkv_hbm, qkv_ref), (down_hbm, down_ref), (embed_hbm, embed_ref))
         )
     ]
-    for load in loads:
-        load.start()
+    weight_loads = [
+        pltpu.make_async_copy(weight_block(z, u), wall_block(z, u), local_sem.at[7])
+        for u in range(units)
+    ]
     barrier = pltpu.get_barrier_semaphore()
     count = 0
     for k in range(n):
@@ -386,218 +410,182 @@
                     device_id_type=MESH,
                 )
                 count += 1
-    if groups == 2:
-        pl.semaphore_signal(barrier, inc=1, device_id={"groups": 1 - y}, device_id_type=MESH)
+    for k in range(n):
+        pl.semaphore_signal(
+            barrier, inc=1, device_id={"groups": 1 - y, "seq": seq_peer(k)}, device_id_type=MESH
+        )
         count += 1
+    for load in token_loads + loads + weight_loads:
+        load.start()
+
+    block = 64
+
+    def norm_quarter(position):
+        index = first_quarters[position]
+        token_loads[position].wait()
+
+        def norm_rows(i, total):
+            at = pl.ds(pl.multiple_of(index * quarter + i * block, block), block)
+            values = tok_ref[at, :].astype(jnp.float32)
+            out = normalize(values, gain_ref[...].reshape(1, width)).astype(jnp.bfloat16)
+            normed[y * 2 + part, index, pl.ds(pl.multiple_of(i * block, block), block), :] = out
+            return total + jnp.sum(values, axis=0, keepdims=True)
+
+        sums[index] = lax.fori_loop(
+            0, quarter // block, norm_rows, jnp.zeros((1, width), jnp.float32)
+        )
+
+    norm_quarter(0)
     pl.semaphore_wait(barrier, count)
 
-    pending = []
-
-    def start(copy, cond=None):
-        if cond is None:
-            copy.start()
-        else:
-            pl.when(cond)(copy.start)
-        pending.append((copy, cond))
-
-    part = lax.rem(z, 2)
-    partner = z + 1 - 2 * part
-    quarter = rows // heads
-
-    def token_rows(member, share):
-        return pl.ds(pl.multiple_of(member * rows + share * quarter, quarter), quarter)
-
-    start(
-        remote(
-            tok_hbm.at[pl.ds(pl.multiple_of(hd * quarter, quarter), quarter)],
-            tok_ref.at[token_rows(part, hd)],
-            send_tok.at[0],
-            recv_tok.at[0],
-            {"seq": partner},
-        )
-    )
-    for d in range(1, n):
-        for i in range(carry):
-            c = chunk(y, i)
-            for side in range(2):
-                goes = z + d < n if side == 0 else z >= d
-                target = lax.min(z + d, n - 1) if side == 0 else lax.max(z - d, 0)
-                at = pl.ds(pl.multiple_of(lax.rem(target, 2) * half_width, half_width), half_width)
-                start(
-                    remote(
-                        w_ref.at[c, :, at],
-                        wall.at[z, c],
-                        send_w.at[side, d - 1, i],
-                        recv_w.at[side, d - 1, i],
-                        {"seq": target},
-                    ),
-                    goes,
-                )
-        if d == 1:
-            for k in range(1, n):
-                start(
-                    remote(
-                        pre_ref,
-                        pre_out.at[z, hd],
-                        send_pre.at[k],
-                        recv_pre.at[k],
-                        {"seq": seq_peer(k)},
-                    )
-                )
+    def send(source, target, sends, receives, device):
+        remote(source, target, sends, receives, device).start()
+
+    def send_weight(k, u):
+        target = ahead(k)
+        send(
+            weight_block(target, u), wall_block(z, u), send_w.at[0], recv_w.at[u], {"seq": target}
+        )
+
+    own_set = y * 2 + part
+    z_set = y * 2 + 1 - part
+    y_set = (1 - y) * 2 + part
+    d_set = (1 - y) * 2 + 1 - part
+
+    def token_copy(which, index, event, part_of, device):
+        slot = normed.at[which, index, pl.ds(part_of * half, half)]
+        return remote(slot, slot, send_tok.at[0], recv_tok.at[event, part_of], device)
+
+    def fan_copy(block_index, share_index, event, device):
+        slot = pre_out.at[block_index, share_index]
+        return remote(slot, slot, send_fan.at[0], recv_fan.at[event, block_index], device)
+
+    for index in range(2):
+        target = jnp.where(
+            at_end,
+            jnp.where(z == 0, 1 + index, n - 2 - index),
+            outward if index == 0 else inner,
+        )
+        send(pre_ref, pre_out.at[z, hd], send_pre.at[0], recv_pre.at[z], {"seq": target})
+    token_copy(own_set, hd, 0, 0, {"seq": partner}).start()
+    for part_of in range(2):
+        token_copy(own_set, hd, 4, part_of, {"groups": 1 - y}).start()
+
+    @pl.when(at_end)
+    def _():
+        token_copy(own_set, hd, 0, 1, {"seq": partner}).start()
+
+    @pl.when(at_end)
+    def _():
+        for u in range(units):
+            send_weight(2, u)
+        for u in range(units):
+            send_weight(1, u)
+            send_weight(3, u)
+
+    @pl.when(inside)
+    def _():
+        for u in range(units):
+            send_weight(1, u)
+
+    pre_out[z, hd] = pre_ref[...]
+    norm_quarter(1)
+
+    def fan_first(b):
+        fan_copy(b, hd, 0, {"head": across}).start()
+        fan_copy(b, hd, 1, {"head": mate}).start()
+
+    def fan_second(b):
+        fan_copy(b, across, 0, {"head": across}).wait_recv()
+        fan_copy(b, across, 2, {"head": mate}).start()
+
+    def stored_block(b, forward=False):
+        slot = pre_out.at[b, hd]
+        remote(slot, slot, send_pre.at[0], recv_pre.at[b], {"seq": partner}).wait_recv()
+        if forward:
+            send(slot, slot, send_pre.at[1], recv_pre.at[b], {"seq": outward})
+        fan_first(b)
+
+    fan_first(z)
+    second_end = jnp.where(z == 0, 2, n - 3)
+
+    @pl.when(at_end)
+    def _():
+        stored_block(partner)
+
+    @pl.when(inside)
+    def _():
+        stored_block(inner, True)
+        token_copy(own_set, hd, 0, 1, {"seq": partner}).start()
+        stored_block(outward)
+
+    norm_quarter(2)
+    norm_quarter(3)
+    for tile in range(tiles):
+        per = heads // tiles
+        means[z, pl.ds(tile, 1), :] = (
+            sum(sums[tile * per + i] for i in range(per)) / patch
+        )
+    for k in range(1, n):
+        send(means.at[z], means.at[z], send_mean.at[0], recv_mean.at[0], {"seq": seq_peer(k)})
     narrow_ref[pl.ds(0, 1), :] = bias_ref[...].reshape(1, narrow)
     narrow_ref[pl.ds(1, 1), :] = sub_ref[...].reshape(1, narrow)
     for j in range(heads):
         wcol_parts[j] = wcol_ref[:, j * narrow : (j + 1) * narrow]
-    for k in range(1, heads):
-        start(
-            remote(
-                wcol_parts.at[head_peer(k)],
-                wcol_out.at[hd],
-                send_aux.at[0, k],
-                recv_aux.at[0, k],
-                {"head": head_peer(k)},
-            )
-        )
-        start(
-            remote(
-                narrow_ref, sub_out.at[hd], send_aux.at[1, k], recv_aux.at[1, k], {"head": head_peer(k)}
-            )
-        )
-        start(
-            remote(
-                pre_ref,
-                pre_out.at[z, hd],
-                send_fan.at[0, k],
-                recv_fan.at[0, k],
-                {"head": head_peer(k)},
-            )
-        )
-    pre_out[z, hd] = pre_ref[...]
     wcol_out[hd] = wcol_parts[hd]
     sub_out[hd] = narrow_ref[...]
 
-    loads[0].wait()
-    block = 64
-
-    def norm_tokens(member, keep_mean):
-        for tile in range(tiles):
-
-            def norm_rows(i, total):
-                at = pl.ds(
-                    pl.multiple_of(member * rows + tile * patch + i * block, block), block
-                )
-                values = tok_ref[at, :].astype(jnp.float32)
-                out = normalize(values, gain_ref[...].reshape(1, width)).astype(jnp.bfloat16)
-                for b in range(n):
-                    normed[b, at, :] = out[:, b * depth : (b + 1) * depth]
-                if keep_mean:
-                    total = total + jnp.sum(values, axis=0, keepdims=True)
-                return total
-
-            total = lax.fori_loop(
-                0, patch // block, norm_rows, jnp.zeros((1, width), jnp.float32)
-            )
-            if keep_mean:
-                means[z, pl.ds(tile, 1), :] = total / patch
-
-    norm_tokens(part, True)
-    for k in range(1, n):
-        start(
-            remote(
-                means.at[z], means.at[z], send_seq.at[0, k], recv_seq.at[0, k], {"seq": seq_peer(k)}
-            )
-        )
-    slot = tok_ref.at[token_rows(1 - part, hd)]
-    remote(slot, slot, send_tok.at[0], recv_tok.at[0], {"seq": partner}).wait_recv()
+    def token_event(which, index, event, part_of, forwards):
+        token_copy(which, index, event, part_of, {"head": mate}).wait_recv()
+        for to, device in forwards:
+            token_copy(which, index, to, part_of, device).start()
+
+    from_z = ((8, {"groups": 1 - y}), (1, {"head": across}), (2, {"head": mate}))
+    token_event(y_set, hd, 4, 0, ((6, {"head": mate}),))
+    fan_second(z)
+
+    @pl.when(inside)
+    def _():
+        stored_block(n - 1 - outward, True)
+        for u in range(units):
+            send_weight(3, u)
+
+    token_event(z_set, hd, 0, 0, from_z)
+    token_event(y_set, hd, 4, 1, ((6, {"head": mate}),))
+
+    @pl.when(at_end)
+    def _():
+        fan_second(partner)
+        stored_block(second_end)
+
+    @pl.when(inside)
+    def _():
+        fan_second(inner)
+        fan_second(outward)
+
+    token_event(z_set, hd, 0, 1, from_z)
+    for part_of in range(2):
+        token_copy(own_set, across, 5, part_of, {"groups": 1 - y}).start()
+
+    @pl.when(at_end)
+    def _():
+        stored_block(n - 1 - z)
+        fan_second(second_end)
+        fan_second(n - 1 - z)
+
+    @pl.when(inside)
+    def _():
+        fan_second(n - 1 - outward)
+
     for k in range(1, heads):
-        start(remote(slot, slot, send_tok.at[k], recv_tok.at[k], {"head": head_peer(k)}))
-
-    columns = 256
-
-    def multiply(weights, owner, first):
-        @pl.loop(0, 2 * (half_width // columns))
-        def _(t):
-            member = lax.rem(t, 2)
-            at = pl.ds(pl.multiple_of(t // 2 * columns, columns), columns)
-            span = pl.ds(pl.multiple_of(member * rows, rows), rows)
-            for g in range(2):
-                if owner is None:
-                    place = part * half_width + t // 2 * columns
-                    w = weights[
-                        pl.ds(g * half, half), :, pl.ds(pl.multiple_of(place, columns), columns)
-                    ]
-                else:
-                    w = weights[owner, pl.ds(g * half, half), :, at]
-                w = w.reshape(depth, columns)
-                x = normed[z if owner is None else owner, span, :]
-                value = jnp.dot(x, w, preferred_element_type=jnp.float32)
-                if first:
-                    acc[g, span, at] = value
-                else:
-                    acc[g, span, at] += value
-
-    def owner_of(side, d):
-        return lax.max(z - d, 0) if side == 0 else lax.min(z + d, n - 1)
-
-    def valid(side, d):
-        return z >= d if side == 0 else z + d < n
-
-    def relay(d):
-        for i in range(carry):
-            c = chunk(y, i)
-            for side in range(2):
-                o = owner_of(side, d)
-                slot = wall.at[o, c]
-                there = valid(side, d)
-                arrive = remote(
-                    slot,
-                    slot,
-                    send_w.at[side, d - 1, i],
-                    recv_w.at[side, d - 1, i],
-                    {"seq": o},
-                )
-                pl.when(there)(arrive.wait_recv)
-                if i < swap:
-                    start(
-                        remote(
-                            slot,
-                            slot,
-                            send_y.at[side, d - 1, i],
-                            recv_y.at[side, d - 1, i],
-                            {"groups": 1 - y},
-                        ),
-                        there,
-                    )
-
-    def finish(d):
-        for side in range(2):
-            o = owner_of(side, d)
-
-            @pl.when(valid(side, d))
-            def _():
-                for i in range(swap):
-                    slot = wall.at[o, chunk(1 - y, i)]
-                    remote(
-                        slot,
-                        slot,
-                        send_y.at[side, d - 1, i],
-                        recv_y.at[side, d - 1, i],
-                        {"groups": 1 - y},
-                    ).wait_recv()
-                multiply(wall, o, False)
-
-    def fan_out():
-        for k in range(1, n):
-            slot = pre_out.at[seq_source(k), hd]
-            remote(
-                slot, slot, send_pre.at[k], recv_pre.at[k], {"seq": seq_peer(k)}
-            ).wait_recv()
-            for j in range(1, heads):
-                start(
-                    remote(
-                        slot, slot, send_fan.at[k, j], recv_fan.at[k, j], {"head": head_peer(j)}
-                    )
-                )
+        send(
+            wcol_parts.at[head_peer(k)],
+            wcol_out.at[hd],
+            send_aux.at[0],
+            recv_aux.at[0],
+            {"head": head_peer(k)},
+        )
+        send(narrow_ref, sub_out.at[hd], send_aux.at[1], recv_aux.at[1], {"head": head_peer(k)})
 
     total_rows = order_ref.shape[0]
     cols, stored_rows = pre_ref.shape
@@ -612,103 +600,148 @@
         variance = sum(jnp.sum(p * p, axis=1, keepdims=True) for p in centered) / features
         scaling = lax.rsqrt(variance + layer_eps)
         return [
-            (p * scaling * slide_ref[...].reshape(1, features)[:, j * cols : (j + 1) * cols]).astype(jnp.bfloat16)
+            (
+                p * scaling * slide_ref[...].reshape(1, features)[:, j * cols : (j + 1) * cols]
+            ).astype(jnp.bfloat16)
             for j, p in enumerate(centered)
         ]
 
     def project(pieces, g):
-        return sum(
-            dot_rows(piece, qkv_parts[g, j])
-            for j, piece in enumerate(pieces)
-        )
-
-    def stored_sequence():
-        for k in range(1, heads):
-            for b in range(n):
-                slot = pre_out.at[seq_source(b), head_source(k)]
-                remote(
-                    slot, slot, send_fan.at[b, k], recv_fan.at[b, k], {"head": head_peer(k)}
-                ).wait_recv()
-        loads[1].wait()
+        return sum(dot_rows(piece, qkv_parts[g, j]) for j, piece in enumerate(pieces))
+
+    step = stored_rows
+
+    def sequence_step(t):
+        at = pl.ds(t * step, step)
+        order = order_ref[at, :]
+        lane = lax.broadcasted_iota(jnp.int32, (step, LANES), 1)
+        wanted = jnp.where(lane < n * tiles, lane // tiles * stored_rows + lane % tiles, -1)
+        fresh_pick[at, :] = jnp.where(order == wanted, 1.0, 0.0).astype(jnp.bfloat16)
+        index = lax.broadcasted_iota(jnp.int32, (step, stored_rows), 1)
+        picks = [
+            jnp.where(order == index + b * stored_rows, 1.0, 0.0).astype(jnp.bfloat16)
+            for b in range(n)
+        ]
+        pieces = []
+        for j in range(heads):
+            piece = sum(dot_rows(picks[b], pre_out[b, j]) for b in range(n))
+            seq_rows[j, at, :] = piece.astype(jnp.bfloat16)
+            pieces.append(piece)
+        normal = row_norm(pieces)
         for g in range(3):
-            for j in range(heads):
-                qkv_parts[g, j] = qkv_ref[g, :, j * cols : (j + 1) * cols]
-        step = stored_rows
-
-        @pl.loop(0, total_rows // step)
-        def _(t):
-            at = pl.ds(pl.multiple_of(t * step, step), step)
-            order = order_ref[at, :]
-            lane = lax.broadcasted_iota(jnp.int32, (step, 128), 1)
-            wanted = jnp.where(
-                lane < n * tiles, lane // tiles * stored_rows + lane % tiles, -1
+            projected[g, at, :] = project(normal, g).astype(jnp.bfloat16)
+
+    loads[0].wait()
+    for g in range(3):
+        for j in range(heads):
+            qkv_parts[g, j] = qkv_ref[g, :, j * cols : (j + 1) * cols]
+    for b in range(n):
+        for event, source in ((1, mate), (2, beyond)):
+            fan_copy(b, source, event, {"head": mate}).wait_recv()
+    relays = (
+        (z_set, across, 1, ((3, {"head": mate}),)),
+        (d_set, hd, 8, ((9, {"head": across}), (10, {"head": mate}))),
+        (y_set, across, 5, ((7, {"head": mate}),)),
+        (d_set, across, 9, ((11, {"head": mate}),)),
+    )
+    for t in range(total_rows // step):
+        sequence_step(t)
+        if t == 0:
+
+            @pl.when(inside)
+            def _():
+                for u in range(units):
+                    send_weight(2, u)
+
+        for which, index, event, forwards in relays[t : t + 1]:
+            for part_of in range(2):
+                token_event(which, index, event, part_of, forwards)
+    for which, index, event, forwards in relays[total_rows // step :]:
+        for part_of in range(2):
+            token_event(which, index, event, part_of, forwards)
+    for which, first in ((z_set, 0), (y_set, 4), (d_set, 8)):
+        for part_of in range(2):
+            token_event(which, mate, first + 2, part_of, ())
+            token_event(which, beyond, first + 3, part_of, ())
+
+    whole = wall.at[:, :, :, pl.ds(0, LANES), :]
+    pltpu.make_async_copy(whole, whole, local_sem.at[7]).wait()
+
+    def multiply(u):
+        r, c = unit(u)
+        others = wall.at[r, c, :, pl.ds(0, (n - 1) * LANES), :]
+        remote(others, others, send_w.at[0], recv_w.at[u], {"seq": partner}).wait_recv()
+
+        @pl.loop(0, 4)
+        def _(s):
+            w = jnp.concatenate([wall[r, c, 0], wall[r, c, 1]], axis=1)
+            x = jnp.concatenate(
+                [
+                    normed[s, :, :, b * depth + r * LANES : b * depth + (r + 1) * LANES].reshape(
+                        rows, LANES
+                    )
+                    for b in range(n)
+                ],
+                axis=1,
             )
-            fresh_pick[at, :] = jnp.where(order == wanted, 1.0, 0.0).astype(jnp.bfloat16)
-            index = lax.broadcasted_iota(jnp.int32, (step, stored_rows), 1)
-            picks = [
-                jnp.where(order == index + b * stored_rows, 1.0, 0.0).astype(jnp.bfloat16)
-                for b in range(n)
-            ]
-            pieces = []
-            for j in range(heads):
-                piece = sum(
-                    dot_rows(picks[b], pre_out[b, j])
-                    for b in range(n)
+            value = jnp.dot(x, w, preferred_element_type=jnp.float32)
+            if r == 0:
+                acc[c, s] = value
+            else:
+                acc[c, s] += value
+
+    def pool(c):
+        for s in range(4):
+            for tile in range(tiles):
+                at = pl.ds(tile * patch, patch)
+                gate = acc[c, s, at, :LANES]
+                hidden = (gate / (1.0 + jnp.exp(-gate)) * acc[c, s, at, LANES:]).astype(
+                    jnp.bfloat16
                 )
-                seq_rows[j, at, :] = piece.astype(jnp.bfloat16)
-                pieces.append(piece)
-            normal = row_norm(pieces)
-            for g in range(3):
-                projected[g, at, :] = project(normal, g).astype(jnp.bfloat16)
-
-    relay(1)
-    fan_out()
-    for k in range(1, heads):
-        slot = tok_ref.at[token_rows(1 - part, head_source(k))]
-        remote(slot, slot, send_tok.at[k], recv_tok.at[k], {"head": head_peer(k)}).wait_recv()
-    norm_tokens(1 - part, False)
-    multiply(w_ref, None, True)
-    for d in range(2, n):
-        if d == n - 1:
-            stored_sequence()
-        relay(d)
-        finish(d - 1)
-    if n == 2:
-        stored_sequence()
-    finish(n - 1)
-
-    for tile in range(2 * tiles):
-
-        @pl.loop(0, half_width // columns)
-        def _(t):
-            at = pl.ds(pl.multiple_of(t * columns, columns), columns)
-            span = pl.ds(tile * patch, patch)
-            gate = acc[0, span, at]
-            hidden = (gate / (1.0 + jnp.exp(-gate)) * acc[1, span, at]).astype(jnp.bfloat16)
-            pooled[z, pl.ds(tile, 1), at] = (
-                jnp.sum(hidden.astype(jnp.float32), axis=0, keepdims=True) / patch
+                pool_mine[s // 2, c, pl.ds((s % 2) * tiles + tile, 1), :] = (
+                    jnp.sum(hidden.astype(jnp.float32), axis=0, keepdims=True) / patch
+                )
+        place = y * n + z
+        pooled[place, c] = pool_mine[y, c]
+        for k in range(n):
+            for other in range(2):
+                if k or other:
+                    yy = 1 - y if other else y
+                    send(
+                        pool_mine.at[yy, c],
+                        pooled.at[place, c],
+                        send_pool.at[c],
+                        recv_pool.at[c],
+                        {"groups": yy, "seq": seq_peer(k)},
+                    )
+
+    for u in range(units):
+        multiply(u)
+        r, c = unit(u)
+        if r == blocks_k - 1:
+            pool(c)
+
+    seen = means.at[pl.ds(0, n - 1)]
+    remote(seen, seen, send_mean.at[0], recv_mean.at[0], {"seq": partner}).wait_recv()
+    for c in range(blocks_c):
+        slot = pooled.at[pl.ds(0, 2 * n - 1), c]
+        remote(slot, slot, send_pool.at[c], recv_pool.at[c], {"seq": partner}).wait_recv()
+    loads[1].wait()
+    loads[2].wait()
+    everyone = jnp.concatenate(
+        [
+            jnp.concatenate(
+                [
+                    pooled[yy * n + b + m, c]
+                    for m in range(2)
+                    for yy in range(2)
+                    for c in range(blocks_c)
+                ],
+                axis=1,
             )
-
-    for k in range(1, n):
-        start(
-            remote(
-                pooled.at[z],
-                pooled.at[z],
-                send_seq.at[1, k],
-                recv_seq.at[1, k],
-                {"seq": seq_peer(k)},
-            )
-        )
-    for k in range(1, n):
-        for which, buffer in ((0, means), (1, pooled)):
-            slot = buffer.at[seq_source(k)]
-            remote(
-                slot, slot, send_seq.at[which, k], recv_seq.at[which, k], {"seq": seq_peer(k)}
-            ).wait_recv()
-    loads[2].wait()
-    loads[3].wait()
-    everyone = jnp.concatenate(
-        [jnp.concatenate([pooled[b], pooled[b + 1]], axis=1) for b in range(0, n, 2)], axis=0
+            for b in range(0, n, 2)
+        ],
+        axis=0,
     )
     high = everyone.astype(jnp.bfloat16)
     rest = everyone - high.astype(jnp.float32)
@@ -717,52 +750,38 @@
     local_part = jnp.zeros((n * tiles, down_ref.shape[1]), jnp.float32)
     for piece in (low, middle, high):
         local_part += jnp.dot(piece, down_ref[...], preferred_element_type=jnp.float32)
-    parts[z, hd] = local_part
+    here = z * heads + hd
+    parts[here] = local_part
     for k in range(n):
         for j in range(heads):
             if k or j:
-                start(
-                    remote(
-                        parts.at[z, hd],
-                        parts.at[z, hd],
-                        send_part.at[k, j],
-                        recv_part.at[k, j],
-                        {"seq": seq_peer(k), "head": head_peer(j)},
-                    )
+                send(
+                    parts.at[here],
+                    parts.at[here],
+                    send_part.at[0],
+                    recv_part.at[0],
+                    {"seq": seq_peer(k), "head": head_peer(j)},
                 )
-    for k in range(n):
-        for j in range(heads):
-            if k or j:
-                slot = parts.at[seq_source(k), head_source(j)]
-                remote(
-                    slot,
-                    slot,
-                    send_part.at[k, j],
-                    recv_part.at[k, j],
-                    {"seq": seq_peer(k), "head": head_peer(j)},
-                ).wait_recv()
+    slot = parts.at[pl.ds(0, n * heads - 1)]
+    remote(slot, slot, send_part.at[0], recv_part.at[0], {"seq": partner}).wait_recv()
     summed = jnp.concatenate(
-        [sum(parts[b, j] for j in range(heads)) for b in range(n)], axis=1
+        [sum(parts[b * heads + j] for j in range(heads)) for b in range(n)], axis=1
     )
     average = jnp.concatenate([means[b] for b in range(n)], axis=0)
-    feature = normalize(average + scale_ref[...].reshape(1, width) * summed, fc_ref[...].reshape(1, width)).astype(jnp.bfloat16)
+    feature = normalize(
+        average + scale_ref[...].reshape(1, width) * summed, fc_ref[...].reshape(1, width)
+    ).astype(jnp.bfloat16)
     fresh = dot_rows(feature, embed_ref[...]) + narrow_ref[pl.ds(0, 1), :]
     new_out[hd] = fresh
     for k in range(1, heads):
-        start(
-            remote(
-                new_out.at[hd], new_out.at[hd], send_new.at[k], recv_new.at[k], {"head": head_peer(k)}
-            )
-        )
-    for k in range(1, heads):
-        peer = {"head": head_peer(k)}
-        source = head_source(k)
-        for slot, sends, receives in (
-            (new_out.at[source], send_new.at[k], recv_new.at[k]),
-            (wcol_out.at[source], send_aux.at[0, k], recv_aux.at[0, k]),
-            (sub_out.at[source], send_aux.at[1, k], recv_aux.at[1, k]),
-        ):
-            remote(slot, slot, sends, receives, peer).wait_recv()
+        send(new_out.at[hd], new_out.at[hd], send_new.at[0], recv_new.at[0], {"head": head_peer(k)})
+    for buffer, receives in (
+        (new_out, recv_new.at[0]),
+        (wcol_out, recv_aux.at[0]),
+        (sub_out, recv_aux.at[1]),
+    ):
+        slot = buffer.at[pl.ds(0, heads - 1)]
+        remote(slot, slot, send_new.at[0], receives, {"head": mate}).wait_recv()
 
     pieces = [new_out[j].astype(jnp.bfloat16).astype(jnp.float32) for j in range(heads)]
     normal = row_norm(pieces)
@@ -885,14 +904,9 @@
 
     slots[hd] = combined.astype(jnp.bfloat16)
     for k in range(1, heads):
-        start(
-            remote(
-                slots.at[hd], slots.at[hd], send_mix.at[k], recv_mix.at[k], {"head": head_peer(k)}
-            )
-        )
-    for k in range(1, heads):
-        slot = slots.at[head_source(k)]
-        remote(slot, slot, send_mix.at[k], recv_mix.at[k], {"head": head_peer(k)}).wait_recv()
+        send(slots.at[hd], slots.at[hd], send_mix.at[0], recv_mix.at[0], {"head": head_peer(k)})
+    slot = slots.at[pl.ds(0, heads - 1)]
+    remote(slot, slot, send_mix.at[0], recv_mix.at[0], {"head": mate}).wait_recv()
     pieces = [slots[j].astype(jnp.float32) for j in range(heads)]
     features = heads * cols
     mean = sum(jnp.sum(p, axis=1, keepdims=True) for p in pieces) / features
@@ -904,11 +918,27 @@
         settled = ((pieces[j] - mean) * scaling * gain).astype(jnp.bfloat16)
         branch += jnp.dot(settled, wcol_out[j], preferred_element_type=jnp.float32)
     out_ref[...] += branch
-    for copy, cond in pending:
-        if cond is None:
-            copy.wait_send()
-        else:
-            pl.when(cond)(copy.wait_send)
+
+    def drain(slot, sends):
+        remote(slot, slot, sends, recv_new.at[0], {"head": mate}).wait_send()
+
+    drain(normed.at[pl.ds(0, 3)], send_tok.at[0])
+    drain(wall.at[:, :, :, pl.ds(0, (n - 1) * LANES), :], send_w.at[0])
+    drain(pre_out.at[0, pl.ds(0, 2)], send_pre.at[0])
+
+    @pl.when(inside)
+    def _():
+        drain(pre_out.at[0, pl.ds(0, 2)], send_pre.at[1])
+
+    drain(pre_out.at[pl.ds(0, 3)], send_fan.at[0])
+    drain(wcol_out.at[pl.ds(0, heads - 1)], send_aux.at[0])
+    drain(sub_out.at[pl.ds(0, heads - 1)], send_aux.at[1])
+    for c in range(blocks_c):
+        drain(pooled.at[pl.ds(0, 2 * n - 1), c], send_pool.at[c])
+    drain(means.at[pl.ds(0, n - 1)], send_mean.at[0])
+    drain(parts.at[pl.ds(0, n * heads - 1)], send_part.at[0])
+    drain(new_out.at[pl.ds(0, heads - 1)], send_new.at[0])
+    drain(slots.at[pl.ds(0, heads - 1)], send_mix.at[0])
 
 
 def near_body(
@@ -943,8 +973,10 @@
     vmem = pl.BlockSpec(memory_space=pltpu.VMEM)
     anywhere = pl.BlockSpec(memory_space=pl.ANY)
     dma = pltpu.SemaphoreType.DMA
-    hops = max(n - 1, 1)
     f32, bf16 = jnp.float32, jnp.bfloat16
+    quarter = rows // heads
+    blocks_k = depth // LANES
+    blocks_c = hidden_width // 4 // LANES
     out = pl.pallas_call(
         functools.partial(encode_kernel, tiles),
         out_shape=jax.ShapeDtypeStruct((block_rows, cols), f32),
@@ -954,7 +986,7 @@
             vmem,
             vmem,
             vmem,
-            vmem,
+            anywhere,
             anywhere,
             anywhere,
             vmem,
@@ -967,7 +999,7 @@
         ],
         out_specs=vmem,
         scratch_shapes=[
-            pltpu.VMEM((2 * rows, width), bf16),
+            pltpu.VMEM((rows, width), bf16),
             pltpu.VMEM(w_down.shape, bf16),
             pltpu.VMEM((cols, width), bf16),
             pltpu.VMEM((3, cols, heads * cols), bf16),
@@ -980,41 +1012,43 @@
             pltpu.VMEM((heads, 2, cols), f32),
             pltpu.VMEM((heads, total_rows, cols), bf16),
             pltpu.VMEM((3, total_rows, cols), bf16),
-            pltpu.VMEM((total_rows, 128), bf16),
-            pltpu.VMEM((4, 128, cols), f32),
+            pltpu.VMEM((total_rows, LANES), bf16),
+            pltpu.VMEM((4, LANES, cols), f32),
             pltpu.VMEM((classes, own_rows, cols), bf16),
             pltpu.VMEM((head_count, classes, own_rows, cols), f32),
-            pltpu.VMEM((head_count, classes, own_rows, 128), f32),
+            pltpu.VMEM((head_count, classes, own_rows, LANES), f32),
             pltpu.VMEM((head_count, classes, own_rows, cols), f32),
-            pltpu.VMEM((head_count, classes, own_rows, 128), f32),
+            pltpu.VMEM((head_count, classes, own_rows, LANES), f32),
             pltpu.VMEM((heads, block_rows, cols), bf16),
-            dma((4,)),
-            dma((heads,)),
-            dma((heads,)),
-            dma((heads,)),
-            dma((heads,)),
-            pltpu.VMEM((n, W_CHUNKS, 2 * depth // W_CHUNKS, hidden_width // 2), bf16),
-            pltpu.VMEM((n, 2 * rows, depth), bf16),
-            pltpu.VMEM((2, 2 * rows, hidden_width // 2), f32),
-            pltpu.VMEM((n, 2 * tiles, hidden_width // 2), f32),
+            pltpu.VMEM((4, heads, quarter, width), bf16),
+            pltpu.VMEM((blocks_k, blocks_c, 2, n * LANES, LANES), bf16),
+            pltpu.VMEM((blocks_c, 4, rows, 2 * LANES), f32),
+            pltpu.VMEM((2, blocks_c, 2 * tiles, LANES), f32),
+            pltpu.VMEM((2 * n, blocks_c, 2 * tiles, LANES), f32),
+            pltpu.VMEM((heads, 1, width), f32),
             pltpu.VMEM((n, tiles, width), f32),
-            pltpu.VMEM((n, heads, n * tiles, w_down.shape[1]), f32),
-            dma((2, hops, W_CHUNKS)),
-            dma((2, hops, W_CHUNKS)),
-            dma((2, hops, W_CHUNKS)),
-            dma((2, hops, W_CHUNKS)),
+            pltpu.VMEM((n * heads, n * tiles, w_down.shape[1]), f32),
+            dma((8,)),
+            dma((1,)),
+            dma((12, 2)),
+            dma((1,)),
+            dma((blocks_k * blocks_c,)),
+            dma((2,)),
             dma((n,)),
-            dma((n,)),
-            dma((n, heads)),
-            dma((n, heads)),
-            dma((2, heads)),
-            dma((2, heads)),
-            dma((2, n)),
-            dma((2, n)),
-            dma((n, heads)),
-            dma((n, heads)),
-            dma((heads,)),
-            dma((heads,)),
+            dma((1,)),
+            dma((3, n)),
+            dma((2,)),
+            dma((2,)),
+            dma((blocks_c,)),
+            dma((blocks_c,)),
+            dma((1,)),
+            dma((1,)),
+            dma((1,)),
+            dma((1,)),
+            dma((1,)),
+            dma((1,)),
+            dma((1,)),
+            dma((1,)),
         ],
         compiler_params=pltpu.CompilerParams(
             collective_id=0, has_side_effects=True, vmem_limit_bytes=58 * 1024 * 1024
@@ -1025,7 +1059,7 @@
         tile_gain,
         layer_scale,
         fc_gain,
-        w_gate_up.reshape(W_CHUNKS, 2 * depth // W_CHUNKS, hidden_width),
+        w_gate_up,
         w_down,
         w_embed.T,
         jnp.pad(pre_emb.T, ((0, 0), (tiles, 0))),
@@ -1041,7 +1075,8 @@
 
 def body(*args):
     total_rows = args[9].shape[0]
-    if total_rows <= SPAN0 and lax.axis_size("seq") % 2 == 0:
+    mesh_fits = all(lax.axis_size(a) == k for a, k in (("groups", 2), ("seq", 4), ("head", 4)))
+    if total_rows <= SPAN0 and mesh_fits:
         return near_body(*args)
     return general_body(*args)
 

time: 109 us -> 86.1 us (0.79)
  Pallas kernels: 101 us -> 78.6 us
    pallas_call x1, Pallas kernels: 101 us -> 78.6 us  [near_body(): pl.pallas_call(functools.partial(encode_kernel, tiles), out_shape=jax.Sha...]
where the time goes in v1:
time: 86.1 us; the launch traced here: 84.9 us
  Pallas kernels  78.6 us (91%)
  local copies, waits for them, and re-layouts  5.63 us (7%)
    pallas_call x1, Pallas kernels, near_body(): pl.pallas_call(functools.partial(encode_kernel, tiles), out_shape=jax.Sha...  78.6 us
    reshape x2, local copies, waits for them, and re-layouts, near_body(): tile_order.reshape(total_rows // classes, classes).T.reshape(total_rows, 1)  2.02 us
    reshape x2, local copies, waits for them, and re-layouts, near_body(): out.reshape(classes, own_rows, cols).transpose(1, 0, 2)  1.9 us

profile of v1, /device:TPU:0, one launch (start us, length us, event | category | flops | bytes accessed | tf_op | source)
XLA Modules:
  0.0 84.9 jit_solution(18357104415038836753)
XLA Ops:
  0.7 0.8 reshape.16
  1.4 0.1 copy.17
  1.5 1.6 %pad.4.pre_ref = bf16[192,256]{1,0:T(8,128)(2,1)} pad(bf16[192,254]{1,0:T(8,128)(2,1)} %bitcast.15, bf16[]{:T(256)} %constant.2.clone.1), padding=0_0x2_0 | pad | bytes 195842 | tf_op jit(solution)/shard_map/jit(_pad)/pad | solution.py:1065
  3.1 1.3 %reshape.20.order_ref = s32[1024,1]{1,0:T(8,128)} reshape(s32[16,64]{1,0:T(8,128)S(1)} %copy.17) | data formatting | bytes 8192 | tf_op jit(solution)/shard_map/reshape | solution.py:972
  4.4 78.6 %shard_map.145 = f32[256,192]{1,0:T(8,128)} custom-call(s32[1]{0:T(128)S(6)} %copy.21.valid_ref, bf16[512,1536]{1,0:T(8,128)(2,1)} %bitcast.9, f32[1536]{0:T(1024)} %gain_ref.1, f32[1536]{0:T(1024)} %scale_ref.1, f32[1536]{0:T(1024)} %fc_ref.1, bf16[2,384,1024]{2,1,0:T(8,128)(2,1)} %w_hbm.1, bf16[1024,384]{1,0:T(8,128)(2,1)} %down_hbm.1, ...), custom_call_target="tpu_custom_call" | custom-call | tf_op jit(solution)/shard_map/pallas_call | solution.py:980
  83.0 1.1 %copy.19 = f32[16,16,192]{2,0,1:T(8,128)S(1)} copy(f32[16,16,192]{2,1,0:T(8,128)} %bitcast.10) | data formatting | bytes 393216 | tf_op jit(solution)/shard_map/reshape | solution.py:1073
  84.1 0.8 copy.20

commit v2 on v1

--- a/solution.py
+++ b/solution.py
@@ -277,23 +277,27 @@
     down_ref,
     embed_ref,
     qkv_ref,
-    qkv_parts,
     wcol_parts,
     narrow_ref,
+    pre_own,
     pre_out,
     new_out,
     wcol_out,
     sub_out,
-    seq_rows,
-    projected,
-    fresh_pick,
-    fresh_rows,
-    own_query,
-    mid_out,
-    mid_mass,
-    far_out,
-    far_mass,
-    slots,
+    sequence,
+    queries,
+    key_rows,
+    value_cols,
+    fresh,
+    keep_rows,
+    keep_cols,
+    slide_col,
+    sub_col,
+    mix_old,
+    mix_query,
+    mix_mass,
+    new_kv,
+    new_mix,
     normed,
     wall,
     acc,
@@ -323,6 +327,8 @@
     recv_new,
     send_mix,
     recv_mix,
+    send_kv,
+    recv_kv,
 ):
     n = lax.axis_size("seq")
     heads = lax.axis_size("head")
@@ -435,6 +441,11 @@
             0, quarter // block, norm_rows, jnp.zeros((1, width), jnp.float32)
         )
 
+    cols, stored_count = pre_ref.shape
+    stored_rows = stored_count + tiles
+    pre_own[...] = jnp.concatenate(
+        [pre_ref[...], jnp.zeros((cols, tiles), jnp.bfloat16)], axis=1
+    )
     norm_quarter(0)
     pl.semaphore_wait(barrier, count)
 
@@ -466,7 +477,7 @@
             jnp.where(z == 0, 1 + index, n - 2 - index),
             outward if index == 0 else inner,
         )
-        send(pre_ref, pre_out.at[z, hd], send_pre.at[0], recv_pre.at[z], {"seq": target})
+        send(pre_own, pre_out.at[z, hd], send_pre.at[0], recv_pre.at[z], {"seq": target})
     token_copy(own_set, hd, 0, 0, {"seq": partner}).start()
     for part_of in range(2):
         token_copy(own_set, hd, 4, part_of, {"groups": 1 - y}).start()
@@ -488,7 +499,7 @@
         for u in range(units):
             send_weight(1, u)
 
-    pre_out[z, hd] = pre_ref[...]
+    pre_out[z, hd] = pre_own[...]
     norm_quarter(1)
 
     def fan_first(b):
@@ -531,9 +542,21 @@
     narrow_ref[pl.ds(0, 1), :] = bias_ref[...].reshape(1, narrow)
     narrow_ref[pl.ds(1, 1), :] = sub_ref[...].reshape(1, narrow)
     for j in range(heads):
-        wcol_parts[j] = wcol_ref[:, j * narrow : (j + 1) * narrow]
+        wcol_parts[j] = wcol_ref[:, j * narrow : (j + 1) * narrow].T
     wcol_out[hd] = wcol_parts[hd]
     sub_out[hd] = narrow_ref[...]
+
+    def column(row):
+        size = row.shape[1]
+        same = lax.broadcasted_iota(jnp.int32, (size, size), 0) == lax.broadcasted_iota(
+            jnp.int32, (size, size), 1
+        )
+        return jnp.sum(jnp.where(same, row, 0.0), axis=1, keepdims=True)
+
+    features = heads * cols
+    for start in range(0, features, LANES):
+        at = pl.ds(start, LANES)
+        slide_col[at, :] = column(slide_ref[...].reshape(1, features)[:, start : start + LANES])
 
     def token_event(which, index, event, part_of, forwards):
         token_copy(which, index, event, part_of, {"head": mate}).wait_recv()
@@ -587,54 +610,95 @@
         )
         send(narrow_ref, sub_out.at[hd], send_aux.at[1], recv_aux.at[1], {"head": head_peer(k)})
 
-    total_rows = order_ref.shape[0]
-    cols, stored_rows = pre_ref.shape
-    classes = DILATION_THIRD
-    class_rows = total_rows // classes
-    own_rows = stored_rows // classes
-
-    def row_norm(pieces):
-        features = heads * cols
-        mean = sum(jnp.sum(p, axis=1, keepdims=True) for p in pieces) / features
-        centered = [p - mean for p in pieces]
-        variance = sum(jnp.sum(p * p, axis=1, keepdims=True) for p in centered) / features
-        scaling = lax.rsqrt(variance + layer_eps)
-        return [
-            (
-                p * scaling * slide_ref[...].reshape(1, features)[:, j * cols : (j + 1) * cols]
-            ).astype(jnp.bfloat16)
-            for j, p in enumerate(centered)
-        ]
-
-    def project(pieces, g):
-        return sum(dot_rows(piece, qkv_parts[g, j]) for j, piece in enumerate(pieces))
-
     step = stored_rows
+    total_rows = n * step
+    limit = valid_ref[0]
+    new_count = n * tiles
+    factor = 1.0 / math.sqrt(HEAD_DIM)
+    head_count = cols // HEAD_DIM
+
+    def multiplicity(first, second, offset):
+        middle = (first % DILATION_SECOND == offset % DILATION_SECOND) & (
+            second % DILATION_SECOND == offset % DILATION_SECOND
+        )
+        distant = (first % DILATION_THIRD == offset % DILATION_THIRD) & (
+            second % DILATION_THIRD == offset % DILATION_THIRD
+        )
+        return 1.0 + jnp.where(middle, 1.0, 0.0) + jnp.where(distant, 1.0, 0.0)
 
     def sequence_step(t):
         at = pl.ds(t * step, step)
-        order = order_ref[at, :]
-        lane = lax.broadcasted_iota(jnp.int32, (step, LANES), 1)
-        wanted = jnp.where(lane < n * tiles, lane // tiles * stored_rows + lane % tiles, -1)
-        fresh_pick[at, :] = jnp.where(order == wanted, 1.0, 0.0).astype(jnp.bfloat16)
-        index = lax.broadcasted_iota(jnp.int32, (step, stored_rows), 1)
-        picks = [
-            jnp.where(order == index + b * stored_rows, 1.0, 0.0).astype(jnp.bfloat16)
-            for b in range(n)
-        ]
-        pieces = []
-        for j in range(heads):
-            piece = sum(dot_rows(picks[b], pre_out[b, j]) for b in range(n))
-            seq_rows[j, at, :] = piece.astype(jnp.bfloat16)
-            pieces.append(piece)
-        normal = row_norm(pieces)
-        for g in range(3):
-            projected[g, at, :] = project(normal, g).astype(jnp.bfloat16)
+        per = step // LANES
+        order = jnp.concatenate([order_ref[pl.ds(t * per + i, 1), :] for i in range(per)], axis=1)
+        label = lax.broadcasted_iota(jnp.int32, (step, step), 0)
+        label = jnp.where(label < stored_count, label + tiles, -n * step)
+        picks = jnp.concatenate(
+            [jnp.where(order == label + b * step, 1.0, 0.0).astype(jnp.bfloat16) for b in range(n)],
+            axis=0,
+        )
+        label = lax.broadcasted_iota(jnp.int32, (LANES, step), 0)
+        wanted = jnp.where(label < new_count, label // tiles * step + label % tiles, -1)
+        found = jnp.where(order == wanted, 1.0, 0.0)
+        fresh[t] = found.astype(jnp.bfloat16)
+        lane = lax.broadcasted_iota(jnp.int32, (1, step), 1) + t * step
+        keep_cols[:, t * step : (t + 1) * step] = jnp.where(
+            lane < limit, 1.0 - jnp.sum(found, axis=0, keepdims=True), 0.0
+        )
+        row = lax.broadcasted_iota(jnp.int32, (step, 1), 0) + t * step
+        keep_rows[at, :] = jnp.where(
+            row < limit, 1.0 - jnp.sum(found.T, axis=1, keepdims=True), 0.0
+        )
+        stored = jnp.concatenate(
+            [jnp.concatenate([pre_out[b, j] for b in range(n)], axis=1) for j in range(heads)],
+            axis=0,
+        )
+        values = jnp.dot(stored, picks, preferred_element_type=jnp.float32)
+        sequence[t] = values.astype(jnp.bfloat16).reshape(heads, cols, step)
+        centered = values - jnp.sum(values, axis=0, keepdims=True) / features
+        variance = jnp.sum(centered * centered, axis=0, keepdims=True) / features
+        normal = (centered * lax.rsqrt(variance + layer_eps) * slide_col[...]).astype(jnp.bfloat16)
+        result = jnp.dot(
+            qkv_ref[...].reshape(3 * cols, features), normal, preferred_element_type=jnp.float32
+        ).astype(jnp.bfloat16)
+        queries[t] = result[:cols]
+        key_rows[at, :] = result[cols : 2 * cols].T
+        value_cols[:, t * step : (t + 1) * step] = result[2 * cols :]
+
+    def attend_stored():
+        query = queries[z]
+        row_head = lax.broadcasted_iota(jnp.int32, (cols, 1), 0) // HEAD_DIM
+        key_at = lax.broadcasted_iota(jnp.int32, (total_rows, 1), 0)
+        query_at = lax.broadcasted_iota(jnp.int32, (1, step), 1) + z * step
+        for h in range(head_count):
+            own = jnp.where(row_head == h, query, jnp.zeros((), jnp.bfloat16))
+            scores = jnp.dot(key_rows[...], own, preferred_element_type=jnp.float32) * factor
+            scores = jnp.where(keep_rows[...] > 0.0, scores, masked_score)
+            peak = jnp.max(scores, axis=0, keepdims=True)
+            weights = jnp.exp(scores - peak) * multiplicity(
+                key_at, query_at, hd * head_count + h
+            )
+            at = slice(h * HEAD_DIM, (h + 1) * HEAD_DIM)
+            values = jnp.concatenate(
+                [value_cols[at, :], jnp.ones((16, total_rows), jnp.bfloat16)], axis=0
+            )
+            total = jnp.dot(
+                values, weights.astype(jnp.bfloat16), preferred_element_type=jnp.float32
+            )
+            mass = total[HEAD_DIM : HEAD_DIM + 1]
+            mix_old[hd, at, :] = (total[:HEAD_DIM] / mass).astype(jnp.bfloat16)
+            mix_mass[hd, h * 8 : (h + 1) * 8, :] = jnp.broadcast_to(peak + jnp.log(mass), (8, step))
+        mix_query[hd] = query
+        for k in range(1, heads):
+            for index, buffer in enumerate((mix_query, mix_mass, mix_old)):
+                send(
+                    buffer.at[hd],
+                    buffer.at[hd],
+                    send_mix.at[index],
+                    recv_mix.at[index],
+                    {"head": head_peer(k)},
+                )
 
     loads[0].wait()
-    for g in range(3):
-        for j in range(heads):
-            qkv_parts[g, j] = qkv_ref[g, :, j * cols : (j + 1) * cols]
     for b in range(n):
         for event, source in ((1, mate), (2, beyond)):
             fan_copy(b, source, event, {"head": mate}).wait_recv()
@@ -653,10 +717,11 @@
                 for u in range(units):
                     send_weight(2, u)
 
-        for which, index, event, forwards in relays[t : t + 1]:
+        for which, index, event, forwards in relays[t : t + 1] if t < 3 else ():
             for part_of in range(2):
                 token_event(which, index, event, part_of, forwards)
-    for which, index, event, forwards in relays[total_rows // step :]:
+    attend_stored()
+    for which, index, event, forwards in relays[3:]:
         for part_of in range(2):
             token_event(which, index, event, part_of, forwards)
     for which, first in ((z_set, 0), (y_set, 4), (d_set, 8)):
@@ -664,6 +729,11 @@
             token_event(which, mate, first + 2, part_of, ())
             token_event(which, beyond, first + 3, part_of, ())
 
+    for buffer, receives in ((wcol_out, recv_aux.at[0]), (sub_out, recv_aux.at[1])):
+        slot = buffer.at[pl.ds(0, heads - 1)]
+        remote(slot, slot, send_new.at[0], receives, {"head": mate}).wait_recv()
+    for j in range(heads):
+        sub_col[pl.ds(j * cols, cols), :] = column(sub_out[j, 1:2])
     whole = wall.at[:, :, :, pl.ds(0, LANES), :]
     pltpu.make_async_copy(whole, whole, local_sem.at[7]).wait()
 
@@ -771,153 +841,127 @@
     feature = normalize(
         average + scale_ref[...].reshape(1, width) * summed, fc_ref[...].reshape(1, width)
     ).astype(jnp.bfloat16)
-    fresh = dot_rows(feature, embed_ref[...]) + narrow_ref[pl.ds(0, 1), :]
-    new_out[hd] = fresh
+    new_out[hd] = (dot_rows(feature, embed_ref[...]) + narrow_ref[pl.ds(0, 1), :]).astype(
+        jnp.bfloat16
+    )
     for k in range(1, heads):
         send(new_out.at[hd], new_out.at[hd], send_new.at[0], recv_new.at[0], {"head": head_peer(k)})
-    for buffer, receives in (
-        (new_out, recv_new.at[0]),
-        (wcol_out, recv_aux.at[0]),
-        (sub_out, recv_aux.at[1]),
-    ):
+
+    def peers(buffer, receives):
         slot = buffer.at[pl.ds(0, heads - 1)]
         remote(slot, slot, send_new.at[0], receives, {"head": mate}).wait_recv()
 
-    pieces = [new_out[j].astype(jnp.bfloat16).astype(jnp.float32) for j in range(heads)]
-    normal = row_norm(pieces)
-    fresh_rows[...] = jnp.zeros(fresh_rows.shape, jnp.float32)
-    filled = pl.ds(0, n * tiles)
-    for g in range(3):
-        fresh_rows[g, filled, :] = project(normal, g)
-    fresh_rows[3, filled, :] = new_out[hd]
-    own_at = pl.ds(pl.multiple_of(z * own_rows, own_rows), own_rows)
-    updated = []
-    for g in range(3):
-        placed = jnp.dot(
-            fresh_pick[...],
-            fresh_rows[g].astype(jnp.bfloat16),
-            preferred_element_type=jnp.float32,
-        )
-        projected[g] = (projected[g].astype(jnp.float32) + placed).astype(jnp.bfloat16)
-    seq_rows[hd] = (
-        seq_rows[hd].astype(jnp.float32)
-        + jnp.dot(
-            fresh_pick[...],
-            fresh_rows[3].astype(jnp.bfloat16),
-            preferred_element_type=jnp.float32,
-        )
+    peers(new_out, recv_new.at[0])
+    fresh_values = jnp.concatenate([new_out[j].astype(jnp.float32) for j in range(heads)], axis=1)
+    normal = normalize(fresh_values, slide_ref[...].reshape(1, features)).astype(jnp.bfloat16)
+    new_query, new_key, new_value = [
+        dot_rows(normal, qkv_ref[g]).astype(jnp.bfloat16) for g in range(3)
+    ]
+    new_kv[hd, 0] = new_key
+    new_kv[hd, 1] = new_value
+    for k in range(1, heads):
+        send(new_kv.at[hd], new_kv.at[hd], send_kv.at[0], recv_kv.at[0], {"head": head_peer(k)})
+    lane_head = lax.broadcasted_iota(jnp.int32, (1, cols), 1) // HEAD_DIM
+    nothing = jnp.zeros((), jnp.bfloat16)
+
+    def by_head(rows_in):
+        return jnp.concatenate(
+            [jnp.where(lane_head == h, rows_in, nothing) for h in range(head_count)], axis=0
+        )
+
+    key_at = lax.broadcasted_iota(jnp.int32, (new_count, total_rows), 1)
+    placed = jnp.concatenate([fresh[t, :new_count].astype(jnp.float32) for t in range(n)], axis=1)
+    new_at = jnp.sum(placed * key_at.astype(jnp.float32), axis=1, keepdims=True).astype(jnp.int32)
+    other = lax.broadcasted_iota(jnp.int32, (1, LANES), 1)
+    new_lane = jnp.sum(
+        jnp.where(other == lax.broadcasted_iota(jnp.int32, (new_count, LANES), 0), new_at, 0),
+        axis=0,
+        keepdims=True,
+    )[:, :new_count]
+
+    many = by_head(new_query)
+    scores = dot_rows(many, key_rows[...]) * factor
+    scores = jnp.where(keep_cols[...] > 0.0, scores, masked_score)
+    recent = dot_rows(many, new_key) * factor
+    recent = jnp.where(new_lane < limit, recent, masked_score)
+    peak = jnp.maximum(
+        jnp.max(scores, axis=1, keepdims=True), jnp.max(recent, axis=1, keepdims=True)
+    )
+    row_at = jnp.concatenate([new_at] * head_count, axis=0)
+    offset = hd * head_count + lax.broadcasted_iota(
+        jnp.int32, (head_count * new_count, 1), 0
+    ) // new_count
+    weights = jnp.exp(scores - peak) * multiplicity(key_at[:1], row_at, offset)
+    recent = jnp.exp(recent - peak) * multiplicity(new_lane, row_at, offset)
+    mass = jnp.sum(weights, axis=1, keepdims=True) + jnp.sum(recent, axis=1, keepdims=True)
+    attended = (
+        dot_rows(weights.astype(jnp.bfloat16), value_cols[...])
+        + jnp.dot(recent.astype(jnp.bfloat16), new_value, preferred_element_type=jnp.float32)
+    ) / mass
+    new_mix[hd] = sum(
+        jnp.where(lane_head == h, attended[h * new_count : (h + 1) * new_count], 0.0)
+        for h in range(head_count)
     ).astype(jnp.bfloat16)
-
-    def class_part(buffer, lead, c):
-        return buffer[lead, pl.ds(pl.multiple_of(c * class_rows, class_rows), class_rows), :]
-
-    for c in range(classes):
-        at = pl.ds(
-            pl.multiple_of(c * class_rows + z * own_rows, own_rows), own_rows
-        )
-        own_query[c] = projected[0, at, :]
-        out_ref[pl.ds(c * own_rows, own_rows), :] = seq_rows[hd, at, :].astype(jnp.float32)
-
-    limit = valid_ref[0]
-    head_count = cols // HEAD_DIM
-    lane_head = lax.broadcasted_iota(jnp.int32, (1, cols), 1) // HEAD_DIM
-    factor = 1.0 / math.sqrt(HEAD_DIM)
-
-    def weigh(queries, keys, values, positions):
+    for k in range(1, heads):
+        send(new_mix.at[hd], new_mix.at[hd], send_kv.at[1], recv_kv.at[1], {"head": head_peer(k)})
+
+    for index, buffer in enumerate((mix_query, mix_mass, mix_old)):
+        peers(buffer, recv_mix.at[index])
+    peers(new_kv, recv_kv.at[0])
+    query_at = lax.broadcasted_iota(jnp.int32, (1, step), 1) + z * step
+    here_fresh = fresh[z, :new_count]
+    known = 1.0 - jnp.sum(here_fresh.astype(jnp.float32), axis=0, keepdims=True)
+    known = jnp.where(query_at < limit, known, 0.0)
+    betas, alphas = [], []
+    for j in range(heads):
         scores = (
-            lax.dot_general(
-                queries, keys, (((1,), (1,)), ((), ())), preferred_element_type=jnp.float32
-            )
+            jnp.dot(by_head(new_kv[j, 0]), mix_query[j], preferred_element_type=jnp.float32)
             * factor
         )
-        scores = jnp.where(positions < limit, scores, masked_score)
-        peak = jnp.max(scores, axis=1, keepdims=True)
-        exponent = jnp.exp(scores - peak)
-        mass = jnp.sum(exponent, axis=1, keepdims=True)
-        weights = (exponent * (1.0 / mass)).astype(jnp.bfloat16)
-        return (
-            jnp.dot(weights, values, preferred_element_type=jnp.float32),
-            peak + jnp.log(mass),
-        )
-
-    block_size = classes * own_rows
-    row_index = lax.broadcasted_iota(jnp.int32, (block_size, 1), 0)
-    row_class = row_index // own_rows
-    row_position = z * block_size + row_index % own_rows * classes + row_class
-    near_lane = lax.broadcasted_iota(jnp.int32, (1, total_rows), 1)
-    near_position = near_lane % class_rows * classes + near_lane // class_rows
-    repeat = classes // DILATION_SECOND
-    mid_lane = lax.broadcasted_iota(jnp.int32, (1, repeat * class_rows), 1)
-    far_lane = lax.broadcasted_iota(jnp.int32, (1, class_rows), 1)
-    mid_out[...] = jnp.zeros(mid_out.shape, jnp.float32)
-    mid_mass[...] = jnp.zeros(mid_mass.shape, jnp.float32)
-    far_out[...] = jnp.zeros(far_out.shape, jnp.float32)
-    far_mass[...] = jnp.zeros(far_mass.shape, jnp.float32)
-    all_queries = own_query[...].reshape(block_size, cols)
-    nothing = jnp.zeros((), jnp.bfloat16)
-    combined = jnp.zeros((block_size, cols), jnp.float32)
-    for j in range(head_count):
-        here = lane_head == j
-        mid_offset = lax.rem(hd * head_count + j, DILATION_SECOND)
-        far_offset = lax.rem(hd * head_count + j, DILATION_THIRD)
-        near, near_log = weigh(
-            jnp.where(here, all_queries, nothing), projected[1], projected[2], near_position
-        )
-        mids = [mid_offset + DILATION_SECOND * t for t in range(repeat)]
-        mid, mid_log = weigh(
-            jnp.where(here, jnp.concatenate([own_query[c] for c in mids], axis=0), nothing),
-            jnp.concatenate([class_part(projected, 1, c) for c in mids], axis=0),
-            jnp.concatenate([class_part(projected, 2, c) for c in mids], axis=0),
-            mid_lane % class_rows * classes
-            + mid_lane // class_rows * DILATION_SECOND
-            + mid_offset,
-        )
-        far, far_log = weigh(
-            jnp.where(here, own_query[far_offset], nothing),
-            class_part(projected, 1, far_offset),
-            class_part(projected, 2, far_offset),
-            far_lane * classes + far_offset,
-        )
-        for t, c in enumerate(mids):
-            mid_out[j, c] = mid[t * own_rows : (t + 1) * own_rows]
-            mid_mass[j, c] = jnp.broadcast_to(
-                mid_log[t * own_rows : (t + 1) * own_rows], (own_rows, 128)
-            )
-        far_out[j, far_offset] = far
-        far_mass[j, far_offset] = jnp.broadcast_to(far_log, (own_rows, 128))
-        mid_log = mid_mass[j].reshape(block_size, 128)[:, :1]
-        far_log = far_mass[j].reshape(block_size, 128)[:, :1]
-        mid_used = row_class % DILATION_SECOND == mid_offset
-        far_used = row_class == far_offset
-        ceiling = jnp.maximum(near_log, jnp.where(mid_used, mid_log, near_log))
-        ceiling = jnp.maximum(ceiling, jnp.where(far_used, far_log, near_log))
-        near_share = jnp.exp(near_log - ceiling)
-        mid_share = jnp.where(mid_used, jnp.exp(mid_log - ceiling), 0.0)
-        far_share = jnp.where(far_used, jnp.exp(far_log - ceiling), 0.0)
-        mixture = (
-            near_share * near
-            + mid_share * mid_out[j].reshape(block_size, cols)
-            + far_share * far_out[j].reshape(block_size, cols)
-        ) / (near_share + mid_share + far_share)
-        combined = jnp.where(here, mixture, combined)
-    combined = jnp.where(row_position < limit, combined, 0.0)
-
-    slots[hd] = combined.astype(jnp.bfloat16)
-    for k in range(1, heads):
-        send(slots.at[hd], slots.at[hd], send_mix.at[0], recv_mix.at[0], {"head": head_peer(k)})
-    slot = slots.at[pl.ds(0, heads - 1)]
-    remote(slot, slot, send_mix.at[0], recv_mix.at[0], {"head": mate}).wait_recv()
-    pieces = [slots[j].astype(jnp.float32) for j in range(heads)]
-    features = heads * cols
-    mean = sum(jnp.sum(p, axis=1, keepdims=True) for p in pieces) / features
-    square = sum(jnp.sum(p * p, axis=1, keepdims=True) for p in pieces) / features
+        scores = jnp.where(row_at < limit, scores, masked_score)
+        offset = j * head_count + lax.broadcasted_iota(
+            jnp.int32, (head_count * new_count, 1), 0
+        ) // new_count
+        grouped = (head_count, new_count, step)
+        scores = scores.reshape(grouped)
+        stored_mass = mix_mass[j].reshape(grouped)
+        ceiling = jnp.maximum(jnp.max(scores, axis=1, keepdims=True), stored_mass)
+        weights = jnp.exp(scores - ceiling) * multiplicity(row_at, query_at, offset).reshape(grouped)
+        old = jnp.exp(stored_mass - ceiling)
+        inverse = known / (old + jnp.sum(weights, axis=1, keepdims=True))
+        betas.append((weights * inverse).reshape(head_count * new_count, step))
+        alphas.append(old * inverse)
+
+    peers(new_mix, recv_kv.at[1])
+    inside_limit = jnp.where(query_at < limit, here_fresh.astype(jnp.float32), 0.0)
+
+    def contract(left, right):
+        return lax.dot_general(
+            left, right, (((0,), (0,)), ((), ())), preferred_element_type=jnp.float32
+        )
+
+    pieces = []
+    for j in range(heads):
+        left = jnp.concatenate([by_head(new_kv[j, 1]), new_mix[j]], axis=0)
+        right = jnp.concatenate([betas[j], inside_limit], axis=0).astype(jnp.bfloat16)
+        share_of = jnp.concatenate(
+            [
+                mix_old[j, h * HEAD_DIM : (h + 1) * HEAD_DIM, :].astype(jnp.float32)
+                * alphas[j][h, :1]
+                for h in range(head_count)
+            ],
+            axis=0,
+        )
+        pieces.append(share_of + contract(left, right))
+    mean = sum(jnp.sum(p, axis=0, keepdims=True) for p in pieces) / features
+    square = sum(jnp.sum(p * p, axis=0, keepdims=True) for p in pieces) / features
     scaling = lax.rsqrt(square - mean * mean + layer_eps)
-    branch = jnp.zeros(out_ref.shape, jnp.float32)
+    branch = sequence[z, hd].astype(jnp.float32) + contract(new_out[hd], here_fresh)
     for j in range(heads):
-        gain = sub_out[j][1:2]
+        gain = sub_col[pl.ds(j * cols, cols), :]
         settled = ((pieces[j] - mean) * scaling * gain).astype(jnp.bfloat16)
-        branch += jnp.dot(settled, wcol_out[j], preferred_element_type=jnp.float32)
-    out_ref[...] += branch
+        branch += jnp.dot(wcol_out[j], settled, preferred_element_type=jnp.float32)
+    out_ref[...] = branch
 
     def drain(slot, sends):
         remote(slot, slot, sends, recv_new.at[0], {"head": mate}).wait_send()
@@ -938,7 +982,10 @@
     drain(means.at[pl.ds(0, n - 1)], send_mean.at[0])
     drain(parts.at[pl.ds(0, n * heads - 1)], send_part.at[0])
     drain(new_out.at[pl.ds(0, heads - 1)], send_new.at[0])
-    drain(slots.at[pl.ds(0, heads - 1)], send_mix.at[0])
+    for index, buffer in enumerate((mix_query, mix_mass, mix_old)):
+        drain(buffer.at[pl.ds(0, heads - 1)], send_mix.at[index])
+    drain(new_kv.at[pl.ds(0, heads - 1)], send_kv.at[0])
+    drain(new_mix.at[pl.ds(0, heads - 1)], send_kv.at[1])
 
 
 def near_body(
@@ -967,9 +1014,6 @@
     head_count = cols // HEAD_DIM
     total_rows = tile_order.shape[0]
     block_rows = total_rows // n
-    classes = DILATION_THIRD
-    own_rows = block_rows // classes
-    by_class = tile_order.reshape(total_rows // classes, classes).T.reshape(total_rows, 1)
     vmem = pl.BlockSpec(memory_space=pltpu.VMEM)
     anywhere = pl.BlockSpec(memory_space=pl.ANY)
     dma = pltpu.SemaphoreType.DMA
@@ -979,7 +1023,7 @@
     blocks_c = hidden_width // 4 // LANES
     out = pl.pallas_call(
         functools.partial(encode_kernel, tiles),
-        out_shape=jax.ShapeDtypeStruct((block_rows, cols), f32),
+        out_shape=jax.ShapeDtypeStruct((cols, block_rows), f32),
         in_specs=[
             pl.BlockSpec(memory_space=pltpu.SMEM),
             anywhere,
@@ -1003,23 +1047,27 @@
             pltpu.VMEM(w_down.shape, bf16),
             pltpu.VMEM((cols, width), bf16),
             pltpu.VMEM((3, cols, heads * cols), bf16),
-            pltpu.VMEM((3, heads, cols, cols), bf16),
             pltpu.VMEM((heads, cols, cols), bf16),
             pltpu.VMEM((2, cols), f32),
+            pltpu.VMEM((cols, block_rows), bf16),
             pltpu.VMEM((n, heads, cols, block_rows), bf16),
-            pltpu.VMEM((heads, n * tiles, cols), f32),
+            pltpu.VMEM((heads, n * tiles, cols), bf16),
             pltpu.VMEM((heads, cols, cols), bf16),
             pltpu.VMEM((heads, 2, cols), f32),
-            pltpu.VMEM((heads, total_rows, cols), bf16),
-            pltpu.VMEM((3, total_rows, cols), bf16),
-            pltpu.VMEM((total_rows, LANES), bf16),
-            pltpu.VMEM((4, LANES, cols), f32),
-            pltpu.VMEM((classes, own_rows, cols), bf16),
-            pltpu.VMEM((head_count, classes, own_rows, cols), f32),
-            pltpu.VMEM((head_count, classes, own_rows, LANES), f32),
-            pltpu.VMEM((head_count, classes, own_rows, cols), f32),
-            pltpu.VMEM((head_count, classes, own_rows, LANES), f32),
-            pltpu.VMEM((heads, block_rows, cols), bf16),
+            pltpu.VMEM((n, heads, cols, block_rows), bf16),
+            pltpu.VMEM((n, cols, block_rows), bf16),
+            pltpu.VMEM((total_rows, cols), bf16),
+            pltpu.VMEM((cols, total_rows), bf16),
+            pltpu.VMEM((n, LANES, block_rows), bf16),
+            pltpu.VMEM((total_rows, 1), f32),
+            pltpu.VMEM((1, total_rows), f32),
+            pltpu.VMEM((heads * cols, 1), f32),
+            pltpu.VMEM((heads * cols, 1), f32),
+            pltpu.VMEM((heads, cols, block_rows), bf16),
+            pltpu.VMEM((heads, cols, block_rows), bf16),
+            pltpu.VMEM((heads, head_count * 8, block_rows), f32),
+            pltpu.VMEM((heads, 2, n * tiles, cols), bf16),
+            pltpu.VMEM((heads, n * tiles, cols), bf16),
             pltpu.VMEM((4, heads, quarter, width), bf16),
             pltpu.VMEM((blocks_k, blocks_c, 2, n * LANES, LANES), bf16),
             pltpu.VMEM((blocks_c, 4, rows, 2 * LANES), f32),
@@ -1047,8 +1095,10 @@
             dma((1,)),
             dma((1,)),
             dma((1,)),
-            dma((1,)),
-            dma((1,)),
+            dma((3,)),
+            dma((3,)),
+            dma((2,)),
+            dma((2,)),
         ],
         compiler_params=pltpu.CompilerParams(
             collective_id=0, has_side_effects=True, vmem_limit_bytes=58 * 1024 * 1024
@@ -1062,15 +1112,15 @@
         w_gate_up,
         w_down,
         w_embed.T,
-        jnp.pad(pre_emb.T, ((0, 0), (tiles, 0))),
+        pre_emb.T,
         w_out,
         embed_bias,
         sub_gain,
-        by_class,
+        tile_order.reshape(total_rows // LANES, LANES),
         slide_gain,
         w_qkv.swapaxes(1, 2),
     )
-    return out.reshape(classes, own_rows, cols).transpose(1, 0, 2).reshape(block_rows, cols)
+    return out.T
 
 
 def body(*args):

time: 86.1 us -> 74.4 us (0.86); the launches traced: 84.9 us -> 74.3 us
  Pallas kernels: 78.6 us -> 72 us
  local copies, waits for them, and re-layouts: 5.63 us -> 1.62 us
    pallas_call x1, Pallas kernels: 78.6 us -> 72 us  [near_body(): pl.pallas_call(functools.partial(encode_kernel, tiles), out_shape=jax.Sha...]
    reshape x4 -> x0, local copies, waits for them, and re-layouts: 3.92 us -> none  [the longest x2 2.02 us: near_body(): tile_order.reshape(total_rows // classes, classes).T.reshape(total_rows, 1)]
    pad x1 -> x0, local copies, waits for them, and re-layouts: 1.65 us -> none  [near_body(): jnp.pad(pre_emb.T, ((0, 0), (tiles, 0)))]
    unnamed x0 -> x1, local copies, waits for them, and re-layouts: none -> 1.62 us
where the time goes in v2:
time: 74.4 us; the launch traced here: 74.3 us
  Pallas kernels  72 us (97%)
  local copies, waits for them, and re-layouts  1.62 us (2%)
    pallas_call x1, Pallas kernels, near_body(): pl.pallas_call(functools.partial(encode_kernel, tiles), out_shape=jax.Sha...  72 us
    unnamed x1, local copies, waits for them, and re-layouts  1.62 us

profile of v2, /device:TPU:0, one launch (start us, length us, event | category | flops | bytes accessed | tf_op | source)
XLA Modules:
  0.0 74.3 jit_solution(15811011606210785731)
XLA Ops:
  0.7 72.0 %shard_map.145 = f32[192,256]{1,0:T(8,128)} custom-call(s32[1]{0:T(128)S(6)} %copy.17.valid_ref, bf16[512,1536]{1,0:T(8,128)(2,1)} %bitcast.6, f32[1536]{0:T(1024)} %gain_ref.1, f32[1536]{0:T(1024)} %scale_ref.1, f32[1536]{0:T(1024)} %fc_ref.1, bf16[2,384,1024]{2,1,0:T(8,128)(2,1)} %w_hbm.1, bf16[1024,384]{1,0:T(8,128)(2,1)} %down_hbm.1, ...), custom_call_target="tpu_custom_call" | custom-call | tf_op jit(solution)/shard_map/pallas_call | solution.py:1024
  72.7 1.6 %copy.18 = f32[256,192]{0,1:T(8,128)} copy(f32[256,192]{0,1:T(8,128)} %bitcast.8) | data formatting | bytes 393216

commit v3 on v2

--- a/solution.py
+++ b/solution.py
@@ -259,20 +259,29 @@
     tiles,
     valid_ref,
     tok_hbm,
+    gain_hbm,
+    scale_hbm,
+    fc_hbm,
+    w_hbm,
+    down_hbm,
+    embed_hbm,
+    pre_hbm,
+    wcol_hbm,
+    bias_hbm,
+    sub_hbm,
+    order_hbm,
+    slide_hbm,
+    qkv_hbm,
+    out_ref,
     gain_ref,
     scale_ref,
     fc_ref,
-    w_hbm,
-    down_hbm,
-    embed_hbm,
     pre_ref,
     wcol_ref,
     bias_ref,
     sub_ref,
     order_ref,
     slide_ref,
-    qkv_hbm,
-    out_ref,
     tok_ref,
     down_ref,
     embed_ref,
@@ -342,7 +351,7 @@
     share = hidden_width // 4
     blocks_k = depth // LANES
     blocks_c = share // LANES
-    narrow = wcol_ref.shape[0]
+    narrow = wcol_hbm.shape[0]
 
     part = lax.rem(z, 2)
     pair = z // 2
@@ -397,7 +406,7 @@
     loads = [
         pltpu.make_async_copy(source, target, local_sem.at[4 + i])
         for i, (source, target) in enumerate(
-            ((qkv_hbm, qkv_ref), (down_hbm, down_ref), (embed_hbm, embed_ref))
+            ((qkv_hbm, qkv_ref), (down_hbm, down_ref), (embed_hbm, embed_ref.at[hd]))
         )
     ]
     weight_loads = [
@@ -421,7 +430,23 @@
             barrier, inc=1, device_id={"groups": 1 - y, "seq": seq_peer(k)}, device_id_type=MESH
         )
         count += 1
-    for load in token_loads + loads + weight_loads:
+    small_loads = [
+        pltpu.make_async_copy(source, target, local_sem.at[8 + i])
+        for i, (source, target) in enumerate(
+            (
+                (pre_hbm, pre_ref),
+                (gain_hbm, gain_ref),
+                (scale_hbm, scale_ref),
+                (fc_hbm, fc_ref),
+                (wcol_hbm, wcol_ref),
+                (bias_hbm, bias_ref),
+                (sub_hbm, sub_ref),
+                (order_hbm, order_ref),
+                (slide_hbm, slide_ref),
+            )
+        )
+    ]
+    for load in token_loads[:1] + small_loads + token_loads[1:] + weight_loads + loads:
         load.start()
 
     block = 64
@@ -441,8 +466,10 @@
             0, quarter // block, norm_rows, jnp.zeros((1, width), jnp.float32)
         )
 
-    cols, stored_count = pre_ref.shape
+    cols, stored_count = pre_hbm.shape
     stored_rows = stored_count + tiles
+    small_loads[0].wait()
+    small_loads[1].wait()
     pre_own[...] = jnp.concatenate(
         [pre_ref[...], jnp.zeros((cols, tiles), jnp.bfloat16)], axis=1
     )
@@ -499,6 +526,21 @@
         for u in range(units):
             send_weight(1, u)
 
+    cols_half = cols // 2
+
+    def embed_half(owner, which):
+        return embed_ref.at[
+            owner, pl.ds(pl.multiple_of(which * cols_half, cols_half), cols_half)
+        ]
+
+    def embed_copy(owner, which, event, device):
+        slot = embed_half(owner, which)
+        return remote(slot, slot, send_new.at[1], recv_new.at[event], device)
+
+    loads[2].wait()
+    own_embed = embed_ref.at[hd]
+    send(own_embed, own_embed, send_new.at[0], recv_new.at[0], {"head": mate})
+    embed_copy(hd, y, 1, {"head": across}).start()
     pre_out[z, hd] = pre_own[...]
     norm_quarter(1)
 
@@ -539,6 +581,8 @@
         )
     for k in range(1, n):
         send(means.at[z], means.at[z], send_mean.at[0], recv_mean.at[0], {"seq": seq_peer(k)})
+    for load in small_loads[2:]:
+        load.wait()
     narrow_ref[pl.ds(0, 1), :] = bias_ref[...].reshape(1, narrow)
     narrow_ref[pl.ds(1, 1), :] = sub_ref[...].reshape(1, narrow)
     for j in range(heads):
@@ -565,51 +609,49 @@
 
     from_z = ((8, {"groups": 1 - y}), (1, {"head": across}), (2, {"head": mate}))
     token_event(y_set, hd, 4, 0, ((6, {"head": mate}),))
-    fan_second(z)
 
     @pl.when(inside)
     def _():
         stored_block(n - 1 - outward, True)
+
+    token_event(z_set, hd, 0, 0, from_z)
+    token_event(y_set, hd, 4, 1, ((6, {"head": mate}),))
+
+    @pl.when(at_end)
+    def _():
+        stored_block(second_end)
+
+    token_event(z_set, hd, 0, 1, (from_z[0], from_z[2]))
+    for part_of in range(2):
+        token_copy(own_set, across, 5, part_of, {"groups": 1 - y}).start()
+
+    @pl.when(at_end)
+    def _():
+        stored_block(n - 1 - z)
+
+    @pl.when(inside)
+    def _():
         for u in range(units):
             send_weight(3, u)
 
-    token_event(z_set, hd, 0, 0, from_z)
-    token_event(y_set, hd, 4, 1, ((6, {"head": mate}),))
+    fan_second(z)
 
     @pl.when(at_end)
     def _():
         fan_second(partner)
-        stored_block(second_end)
+        fan_second(second_end)
 
     @pl.when(inside)
     def _():
         fan_second(inner)
         fan_second(outward)
-
-    token_event(z_set, hd, 0, 1, from_z)
+        for u in range(units):
+            send_weight(2, u)
+
+    token_copy(z_set, hd, 1, 1, {"head": across}).start()
     for part_of in range(2):
-        token_copy(own_set, across, 5, part_of, {"groups": 1 - y}).start()
-
-    @pl.when(at_end)
-    def _():
-        stored_block(n - 1 - z)
-        fan_second(second_end)
-        fan_second(n - 1 - z)
-
-    @pl.when(inside)
-    def _():
-        fan_second(n - 1 - outward)
-
-    for k in range(1, heads):
-        send(
-            wcol_parts.at[head_peer(k)],
-            wcol_out.at[hd],
-            send_aux.at[0],
-            recv_aux.at[0],
-            {"head": head_peer(k)},
-        )
-        send(narrow_ref, sub_out.at[hd], send_aux.at[1], recv_aux.at[1], {"head": head_peer(k)})
-
+        token_event(d_set, hd, 8, part_of, ((9, {"head": across}), (10, {"head": mate})))
+    fan_second(jnp.where(at_end, n - 1 - z, n - 1 - outward))
     step = stored_rows
     total_rows = n * step
     limit = valid_ref[0]
@@ -702,75 +744,89 @@
     for b in range(n):
         for event, source in ((1, mate), (2, beyond)):
             fan_copy(b, source, event, {"head": mate}).wait_recv()
-    relays = (
-        (z_set, across, 1, ((3, {"head": mate}),)),
-        (d_set, hd, 8, ((9, {"head": across}), (10, {"head": mate}))),
-        (y_set, across, 5, ((7, {"head": mate}),)),
-        (d_set, across, 9, ((11, {"head": mate}),)),
-    )
-    for t in range(total_rows // step):
+    for t in range(n):
         sequence_step(t)
-        if t == 0:
-
-            @pl.when(inside)
-            def _():
-                for u in range(units):
-                    send_weight(2, u)
-
-        for which, index, event, forwards in relays[t : t + 1] if t < 3 else ():
+        if t == 1:
+            embed_copy(across, y, 1, {"head": across}).wait_recv()
+            embed_copy(across, y, 2, {"groups": 1 - y}).start()
+            embed_copy(across, y, 3, {"head": mate}).start()
+        if t in (0, n - 2):
+            which, index, event = (z_set, across, 1) if t == 0 else (y_set, across, 5)
             for part_of in range(2):
-                token_event(which, index, event, part_of, forwards)
+                token_event(which, index, event, part_of, ((event + 2, {"head": mate}),))
     attend_stored()
-    for which, index, event, forwards in relays[3:]:
-        for part_of in range(2):
-            token_event(which, index, event, part_of, forwards)
+    for k in range(1, heads):
+        send(
+            wcol_parts.at[head_peer(k)],
+            wcol_out.at[hd],
+            send_aux.at[0],
+            recv_aux.at[0],
+            {"head": head_peer(k)},
+        )
+        send(narrow_ref, sub_out.at[hd], send_aux.at[1], recv_aux.at[1], {"head": head_peer(k)})
+    for part_of in range(2):
+        token_event(d_set, across, 9, part_of, ((11, {"head": mate}),))
+    embed_copy(across, 1 - y, 2, {"groups": 1 - y}).wait_recv()
+    embed_copy(across, 1 - y, 4, {"head": mate}).start()
     for which, first in ((z_set, 0), (y_set, 4), (d_set, 8)):
         for part_of in range(2):
             token_event(which, mate, first + 2, part_of, ())
             token_event(which, beyond, first + 3, part_of, ())
 
-    for buffer, receives in ((wcol_out, recv_aux.at[0]), (sub_out, recv_aux.at[1])):
-        slot = buffer.at[pl.ds(0, heads - 1)]
-        remote(slot, slot, send_new.at[0], receives, {"head": mate}).wait_recv()
-    for j in range(heads):
-        sub_col[pl.ds(j * cols, cols), :] = column(sub_out[j, 1:2])
     whole = wall.at[:, :, :, pl.ds(0, LANES), :]
     pltpu.make_async_copy(whole, whole, local_sem.at[7]).wait()
 
-    def multiply(u):
+    def arrived(u):
         r, c = unit(u)
         others = wall.at[r, c, :, pl.ds(0, (n - 1) * LANES), :]
         remote(others, others, send_w.at[0], recv_w.at[u], {"seq": partner}).wait_recv()
 
+    def gathered(r, chosen):
+        return jnp.concatenate([wall[r, c, g] for c in chosen for g in range(2)], axis=1)
+
+    def token_block(s, r):
+        return jnp.concatenate(
+            [
+                normed[s, :, :, b * depth + r * LANES : b * depth + (r + 1) * LANES].reshape(
+                    rows, LANES
+                )
+                for b in range(n)
+            ],
+            axis=1,
+        )
+
+    def multiply(r):
+        for c in range(blocks_c):
+            arrived(r * blocks_c + c)
+        w = gathered(r, range(blocks_c))
+
         @pl.loop(0, 4)
         def _(s):
-            w = jnp.concatenate([wall[r, c, 0], wall[r, c, 1]], axis=1)
-            x = jnp.concatenate(
-                [
-                    normed[s, :, :, b * depth + r * LANES : b * depth + (r + 1) * LANES].reshape(
-                        rows, LANES
-                    )
-                    for b in range(n)
-                ],
-                axis=1,
+            value = jnp.dot(token_block(s, r), w, preferred_element_type=jnp.float32)
+            if r == 0:
+                acc[s] = value
+            else:
+                acc[s] += value
+
+    def pool(c):
+        r = blocks_k - 1
+        arrived(r * blocks_c + c)
+        w = gathered(r, (c,))
+
+        @pl.loop(0, 4)
+        def _(s):
+            value = acc[s, :, 2 * c * LANES : 2 * (c + 1) * LANES] + jnp.dot(
+                token_block(s, r), w, preferred_element_type=jnp.float32
             )
-            value = jnp.dot(x, w, preferred_element_type=jnp.float32)
-            if r == 0:
-                acc[c, s] = value
-            else:
-                acc[c, s] += value
-
-    def pool(c):
-        for s in range(4):
+            gate = value[:, :LANES]
+            hidden = (gate / (1.0 + jnp.exp(-gate)) * value[:, LANES:]).astype(jnp.bfloat16)
+            hidden = hidden.astype(jnp.float32)
             for tile in range(tiles):
-                at = pl.ds(tile * patch, patch)
-                gate = acc[c, s, at, :LANES]
-                hidden = (gate / (1.0 + jnp.exp(-gate)) * acc[c, s, at, LANES:]).astype(
-                    jnp.bfloat16
+                pool_mine[s // 2, c, pl.ds(s % 2 * tiles + tile, 1), :] = (
+                    jnp.sum(hidden[tile * patch : (tile + 1) * patch], axis=0, keepdims=True)
+                    / patch
                 )
-                pool_mine[s // 2, c, pl.ds((s % 2) * tiles + tile, 1), :] = (
-                    jnp.sum(hidden.astype(jnp.float32), axis=0, keepdims=True) / patch
-                )
+
         place = y * n + z
         pooled[place, c] = pool_mine[y, c]
         for k in range(n):
@@ -785,11 +841,10 @@
                         {"groups": yy, "seq": seq_peer(k)},
                     )
 
-    for u in range(units):
-        multiply(u)
-        r, c = unit(u)
-        if r == blocks_k - 1:
-            pool(c)
+    for r in range(blocks_k - 1):
+        multiply(r)
+    for c in range(blocks_c):
+        pool(c)
 
     seen = means.at[pl.ds(0, n - 1)]
     remote(seen, seen, send_mean.at[0], recv_mean.at[0], {"seq": partner}).wait_recv()
@@ -797,7 +852,6 @@
         slot = pooled.at[pl.ds(0, 2 * n - 1), c]
         remote(slot, slot, send_pool.at[c], recv_pool.at[c], {"seq": partner}).wait_recv()
     loads[1].wait()
-    loads[2].wait()
     everyone = jnp.concatenate(
         [
             jnp.concatenate(
@@ -821,7 +875,7 @@
     for piece in (low, middle, high):
         local_part += jnp.dot(piece, down_ref[...], preferred_element_type=jnp.float32)
     here = z * heads + hd
-    parts[here] = local_part
+    parts[here] = local_part.astype(jnp.bfloat16)
     for k in range(n):
         for j in range(heads):
             if k or j:
@@ -832,27 +886,38 @@
                     recv_part.at[0],
                     {"seq": seq_peer(k), "head": head_peer(j)},
                 )
+    for buffer, receives in ((wcol_out, recv_aux.at[0]), (sub_out, recv_aux.at[1])):
+        slot = buffer.at[pl.ds(0, heads - 1)]
+        remote(slot, slot, send_aux.at[0], receives, {"head": mate}).wait_recv()
+    for j in range(heads):
+        sub_col[pl.ds(j * cols, cols), :] = column(sub_out[j, 1:2])
     slot = parts.at[pl.ds(0, n * heads - 1)]
     remote(slot, slot, send_part.at[0], recv_part.at[0], {"seq": partner}).wait_recv()
+    remote(own_embed, own_embed, send_new.at[0], recv_new.at[0], {"head": mate}).wait_recv()
+    for which, event in ((y, 3), (1 - y, 4)):
+        embed_copy(beyond, which, event, {"head": mate}).wait_recv()
     summed = jnp.concatenate(
-        [sum(parts[b * heads + j] for j in range(heads)) for b in range(n)], axis=1
+        [
+            sum(parts[b * heads + j].astype(jnp.float32) for j in range(heads))
+            for b in range(n)
+        ],
+        axis=1,
     )
     average = jnp.concatenate([means[b] for b in range(n)], axis=0)
     feature = normalize(
         average + scale_ref[...].reshape(1, width) * summed, fc_ref[...].reshape(1, width)
     ).astype(jnp.bfloat16)
-    new_out[hd] = (dot_rows(feature, embed_ref[...]) + narrow_ref[pl.ds(0, 1), :]).astype(
-        jnp.bfloat16
-    )
-    for k in range(1, heads):
-        send(new_out.at[hd], new_out.at[hd], send_new.at[0], recv_new.at[0], {"head": head_peer(k)})
+    table = embed_ref[...].reshape(heads * cols, width)
+    shift = jnp.concatenate([sub_out[j, 0:1] for j in range(heads)], axis=1)
+    fresh_values = (dot_rows(feature, table) + shift).astype(jnp.bfloat16)
+    for j in range(heads):
+        new_out[j] = fresh_values[:, j * cols : (j + 1) * cols]
+    fresh_values = fresh_values.astype(jnp.float32)
 
     def peers(buffer, receives):
         slot = buffer.at[pl.ds(0, heads - 1)]
-        remote(slot, slot, send_new.at[0], receives, {"head": mate}).wait_recv()
-
-    peers(new_out, recv_new.at[0])
-    fresh_values = jnp.concatenate([new_out[j].astype(jnp.float32) for j in range(heads)], axis=1)
+        remote(slot, slot, send_aux.at[0], receives, {"head": mate}).wait_recv()
+
     normal = normalize(fresh_values, slide_ref[...].reshape(1, features)).astype(jnp.bfloat16)
     new_query, new_key, new_value = [
         dot_rows(normal, qkv_ref[g]).astype(jnp.bfloat16) for g in range(3)
@@ -981,7 +1046,8 @@
         drain(pooled.at[pl.ds(0, 2 * n - 1), c], send_pool.at[c])
     drain(means.at[pl.ds(0, n - 1)], send_mean.at[0])
     drain(parts.at[pl.ds(0, n * heads - 1)], send_part.at[0])
-    drain(new_out.at[pl.ds(0, heads - 1)], send_new.at[0])
+    drain(own_embed, send_new.at[0])
+    drain(embed_ref.at[pl.ds(0, 2)], send_new.at[1])
     for index, buffer in enumerate((mix_query, mix_mass, mix_old)):
         drain(buffer.at[pl.ds(0, heads - 1)], send_mix.at[index])
     drain(new_kv.at[pl.ds(0, heads - 1)], send_kv.at[0])
@@ -1023,29 +1089,22 @@
     blocks_c = hidden_width // 4 // LANES
     out = pl.pallas_call(
         functools.partial(encode_kernel, tiles),
-        out_shape=jax.ShapeDtypeStruct((cols, block_rows), f32),
-        in_specs=[
-            pl.BlockSpec(memory_space=pltpu.SMEM),
-            anywhere,
-            vmem,
-            vmem,
-            vmem,
-            anywhere,
-            anywhere,
-            anywhere,
-            vmem,
-            vmem,
-            vmem,
-            vmem,
-            vmem,
-            vmem,
-            anywhere,
-        ],
+        out_shape=pltpu.VMEM((cols, block_rows), f32),
+        in_specs=[pl.BlockSpec(memory_space=pltpu.SMEM)] + [anywhere] * 14,
         out_specs=vmem,
         scratch_shapes=[
+            pltpu.VMEM((width,), f32),
+            pltpu.VMEM((width,), f32),
+            pltpu.VMEM((width,), f32),
+            pltpu.VMEM((cols, block_rows - tiles), bf16),
+            pltpu.VMEM((cols, heads * cols), bf16),
+            pltpu.VMEM((cols,), f32),
+            pltpu.VMEM((cols,), f32),
+            pltpu.VMEM((total_rows // LANES, LANES), jnp.int32),
+            pltpu.VMEM((heads * cols,), f32),
             pltpu.VMEM((rows, width), bf16),
             pltpu.VMEM(w_down.shape, bf16),
-            pltpu.VMEM((cols, width), bf16),
+            pltpu.VMEM((heads, cols, width), bf16),
             pltpu.VMEM((3, cols, heads * cols), bf16),
             pltpu.VMEM((heads, cols, cols), bf16),
             pltpu.VMEM((2, cols), f32),
@@ -1070,13 +1129,13 @@
             pltpu.VMEM((heads, n * tiles, cols), bf16),
             pltpu.VMEM((4, heads, quarter, width), bf16),
             pltpu.VMEM((blocks_k, blocks_c, 2, n * LANES, LANES), bf16),
-            pltpu.VMEM((blocks_c, 4, rows, 2 * LANES), f32),
+            pltpu.VMEM((4, rows, blocks_c * 2 * LANES), f32),
             pltpu.VMEM((2, blocks_c, 2 * tiles, LANES), f32),
             pltpu.VMEM((2 * n, blocks_c, 2 * tiles, LANES), f32),
             pltpu.VMEM((heads, 1, width), f32),
             pltpu.VMEM((n, tiles, width), f32),
-            pltpu.VMEM((n * heads, n * tiles, w_down.shape[1]), f32),
-            dma((8,)),
+            pltpu.VMEM((n * heads, n * tiles, w_down.shape[1]), bf16),
+            dma((17,)),
             dma((1,)),
             dma((12, 2)),
             dma((1,)),
@@ -1093,8 +1152,8 @@
             dma((1,)),
             dma((1,)),
             dma((1,)),
-            dma((1,)),
-            dma((1,)),
+            dma((2,)),
+            dma((5,)),
             dma((3,)),
             dma((3,)),
             dma((2,)),

time: 74.4 us -> 68.8 us (0.925)
  Pallas kernels: 72 us -> 67.3 us
  local copies, waits for them, and re-layouts: 1.62 us -> 0.68 us
    pallas_call x1, Pallas kernels: 72 us -> 67.3 us  [near_body(): pl.pallas_call(functools.partial(encode_kernel, tiles), out_shape=pltpu.V...]
    unnamed x1, local copies, waits for them, and re-layouts: 1.62 us -> 0.68 us
where the time goes in v3:
time: 68.8 us; the launch traced here: 68.7 us
  Pallas kernels  67.3 us (98%)
    pallas_call x1, Pallas kernels, near_body(): pl.pallas_call(functools.partial(encode_kernel, tiles), out_shape=pltpu.V...  67.3 us

profile of v3, /device:TPU:0, one launch (start us, length us, event | category | flops | bytes accessed | tf_op | source)
XLA Modules:
  0.0 68.7 jit_solution(2312268547484346562)
XLA Ops:
  0.7 67.3 %shard_map.145 = f32[192,256]{1,0:T(8,128)S(1)} custom-call(s32[1]{0:T(128)S(6)} %copy.18.valid_ref, bf16[512,1536]{1,0:T(8,128)(2,1)} %bitcast.7, f32[1536]{0:T(1024)} %gain_hbm.1, f32[1536]{0:T(1024)} %scale_hbm.1, f32[1536]{0:T(1024)} %fc_hbm.1, bf16[2,384,1024]{2,1,0:T(8,128)(2,1)} %w_hbm.1, bf16[1024,384]{1,0:T(8,128)(2,1)} %down_hbm.1, ...), custom_call_target="tpu_custom_call" | custom-call | tf_op jit(solution)/shard_map/pallas_call | solution.py:1090
  68.0 0.7 copy.17

commit v4 on v3

--- a/solution.py
+++ b/solution.py
@@ -310,6 +310,7 @@
     normed,
     wall,
     acc,
+    pool_parts,
     pool_mine,
     pooled,
     sums,
@@ -318,6 +319,7 @@
     local_sem,
     send_tok,
     recv_tok,
+    recv_mate,
     send_w,
     recv_w,
     send_pre,
@@ -473,7 +475,11 @@
     pre_own[...] = jnp.concatenate(
         [pre_ref[...], jnp.zeros((cols, tiles), jnp.bfloat16)], axis=1
     )
-    norm_quarter(0)
+
+    @pl.when(z < 2)
+    def _():
+        norm_quarter(0)
+
     pl.semaphore_wait(barrier, count)
 
     def send(source, target, sends, receives, device):
@@ -485,6 +491,21 @@
             weight_block(target, u), wall_block(z, u), send_w.at[0], recv_w.at[u], {"seq": target}
         )
 
+    def end_weights(r):
+        for c in range(blocks_c):
+            send_weight(1, r * blocks_c + c)
+            send_weight(3, r * blocks_c + c)
+
+    def paced_weights(r):
+        @pl.when(at_end)
+        def _():
+            end_weights(r)
+
+        @pl.when(inside)
+        def _():
+            for c in range(blocks_c):
+                send_weight(2, r * blocks_c + c)
+
     own_set = y * 2 + part
     z_set = y * 2 + 1 - part
     y_set = (1 - y) * 2 + part
@@ -492,11 +513,13 @@
 
     def token_copy(which, index, event, part_of, device):
         slot = normed.at[which, index, pl.ds(part_of * half, half)]
-        return remote(slot, slot, send_tok.at[0], recv_tok.at[event, part_of], device)
+        receives = recv_mate.at[0] if event % 4 > 1 else recv_tok.at[event // 4 * 2 + event % 4, part_of]
+        return remote(slot, slot, send_tok.at[0], receives, device)
 
     def fan_copy(block_index, share_index, event, device):
         slot = pre_out.at[block_index, share_index]
-        return remote(slot, slot, send_fan.at[0], recv_fan.at[event, block_index], device)
+        receives = recv_mate.at[1] if event else recv_fan.at[block_index]
+        return remote(slot, slot, send_fan.at[0], receives, device)
 
     for index in range(2):
         target = jnp.where(
@@ -505,6 +528,11 @@
             outward if index == 0 else inner,
         )
         send(pre_own, pre_out.at[z, hd], send_pre.at[0], recv_pre.at[z], {"seq": target})
+
+    @pl.when(z >= 2)
+    def _():
+        norm_quarter(0)
+
     token_copy(own_set, hd, 0, 0, {"seq": partner}).start()
     for part_of in range(2):
         token_copy(own_set, hd, 4, part_of, {"groups": 1 - y}).start()
@@ -517,9 +545,7 @@
     def _():
         for u in range(units):
             send_weight(2, u)
-        for u in range(units):
-            send_weight(1, u)
-            send_weight(3, u)
+        end_weights(0)
 
     @pl.when(inside)
     def _():
@@ -645,12 +671,13 @@
     def _():
         fan_second(inner)
         fan_second(outward)
-        for u in range(units):
-            send_weight(2, u)
+        for c in range(blocks_c):
+            send_weight(2, c)
 
     token_copy(z_set, hd, 1, 1, {"head": across}).start()
     for part_of in range(2):
         token_event(d_set, hd, 8, part_of, ((9, {"head": across}), (10, {"head": mate})))
+    paced_weights(1)
     fan_second(jnp.where(at_end, n - 1 - z, n - 1 - outward))
     step = stored_rows
     total_rows = n * step
@@ -741,12 +768,13 @@
                 )
 
     loads[0].wait()
-    for b in range(n):
-        for event, source in ((1, mate), (2, beyond)):
-            fan_copy(b, source, event, {"head": mate}).wait_recv()
+    slot = pre_out.at[:, pl.ds(0, 2)]
+    remote(slot, slot, send_fan.at[0], recv_mate.at[1], {"head": mate}).wait_recv()
     for t in range(n):
         sequence_step(t)
         if t == 1:
+            for r in range(2, blocks_k):
+                paced_weights(r)
             embed_copy(across, y, 1, {"head": across}).wait_recv()
             embed_copy(across, y, 2, {"groups": 1 - y}).start()
             embed_copy(across, y, 3, {"head": mate}).start()
@@ -754,7 +782,6 @@
             which, index, event = (z_set, across, 1) if t == 0 else (y_set, across, 5)
             for part_of in range(2):
                 token_event(which, index, event, part_of, ((event + 2, {"head": mate}),))
-    attend_stored()
     for k in range(1, heads):
         send(
             wcol_parts.at[head_peer(k)],
@@ -764,15 +791,13 @@
             {"head": head_peer(k)},
         )
         send(narrow_ref, sub_out.at[hd], send_aux.at[1], recv_aux.at[1], {"head": head_peer(k)})
+    attend_stored()
     for part_of in range(2):
         token_event(d_set, across, 9, part_of, ((11, {"head": mate}),))
     embed_copy(across, 1 - y, 2, {"groups": 1 - y}).wait_recv()
     embed_copy(across, 1 - y, 4, {"head": mate}).start()
-    for which, first in ((z_set, 0), (y_set, 4), (d_set, 8)):
-        for part_of in range(2):
-            token_event(which, mate, first + 2, part_of, ())
-            token_event(which, beyond, first + 3, part_of, ())
-
+    slot = normed.at[pl.ds(0, 3), pl.ds(0, 2)]
+    remote(slot, slot, send_tok.at[0], recv_mate.at[0], {"head": mate}).wait_recv()
     whole = wall.at[:, :, :, pl.ds(0, LANES), :]
     pltpu.make_async_copy(whole, whole, local_sem.at[7]).wait()
 
@@ -808,59 +833,55 @@
             else:
                 acc[s] += value
 
-    def pool(c):
+    def pool():
         r = blocks_k - 1
-        arrived(r * blocks_c + c)
-        w = gathered(r, (c,))
+        for c in range(blocks_c):
+            arrived(r * blocks_c + c)
+        w = gathered(r, range(blocks_c))
 
         @pl.loop(0, 4)
         def _(s):
-            value = acc[s, :, 2 * c * LANES : 2 * (c + 1) * LANES] + jnp.dot(
-                token_block(s, r), w, preferred_element_type=jnp.float32
-            )
-            gate = value[:, :LANES]
-            hidden = (gate / (1.0 + jnp.exp(-gate)) * value[:, LANES:]).astype(jnp.bfloat16)
-            hidden = hidden.astype(jnp.float32)
-            for tile in range(tiles):
-                pool_mine[s // 2, c, pl.ds(s % 2 * tiles + tile, 1), :] = (
-                    jnp.sum(hidden[tile * patch : (tile + 1) * patch], axis=0, keepdims=True)
-                    / patch
-                )
-
+            value = acc[s] + jnp.dot(token_block(s, r), w, preferred_element_type=jnp.float32)
+            for c in range(blocks_c):
+                gate = value[:, 2 * c * LANES : (2 * c + 1) * LANES]
+                raised = value[:, (2 * c + 1) * LANES : (2 * c + 2) * LANES]
+                hidden = (gate / (1.0 + jnp.exp(-gate)) * raised).astype(jnp.bfloat16)
+                hidden = hidden.astype(jnp.float32)
+                for tile in range(tiles):
+                    pool_parts[s // 2, c, pl.ds(s % 2 * tiles + tile, 1), :] = (
+                        jnp.sum(hidden[tile * patch : (tile + 1) * patch], axis=0, keepdims=True)
+                        / patch
+                    )
+
+        for yy in range(2):
+            pool_mine[yy] = jnp.concatenate([pool_parts[yy, c] for c in range(blocks_c)], axis=1)
         place = y * n + z
-        pooled[place, c] = pool_mine[y, c]
-        for k in range(n):
+        pooled[place] = pool_mine[y]
+        for k in reversed(range(n)):
             for other in range(2):
                 if k or other:
                     yy = 1 - y if other else y
                     send(
-                        pool_mine.at[yy, c],
-                        pooled.at[place, c],
-                        send_pool.at[c],
-                        recv_pool.at[c],
-                        {"groups": yy, "seq": seq_peer(k)},
+                        pool_mine.at[yy],
+                        pooled.at[place],
+                        send_pool.at[0],
+                        recv_pool.at[0],
+                        {"groups": yy, "seq": ahead(k)},
                     )
 
     for r in range(blocks_k - 1):
         multiply(r)
-    for c in range(blocks_c):
-        pool(c)
+    pool()
 
     seen = means.at[pl.ds(0, n - 1)]
     remote(seen, seen, send_mean.at[0], recv_mean.at[0], {"seq": partner}).wait_recv()
-    for c in range(blocks_c):
-        slot = pooled.at[pl.ds(0, 2 * n - 1), c]
-        remote(slot, slot, send_pool.at[c], recv_pool.at[c], {"seq": partner}).wait_recv()
+    slot = pooled.at[pl.ds(0, 2 * n - 1)]
+    remote(slot, slot, send_pool.at[0], recv_pool.at[0], {"seq": partner}).wait_recv()
     loads[1].wait()
     everyone = jnp.concatenate(
         [
             jnp.concatenate(
-                [
-                    pooled[yy * n + b + m, c]
-                    for m in range(2)
-                    for yy in range(2)
-                    for c in range(blocks_c)
-                ],
+                [pooled[yy * n + b + m] for m in range(2) for yy in range(2)],
                 axis=1,
             )
             for b in range(0, n, 2)
@@ -871,20 +892,23 @@
     rest = everyone - high.astype(jnp.float32)
     middle = rest.astype(jnp.bfloat16)
     low = (rest - middle.astype(jnp.float32)).astype(jnp.bfloat16)
-    local_part = jnp.zeros((n * tiles, down_ref.shape[1]), jnp.float32)
-    for piece in (low, middle, high):
-        local_part += jnp.dot(piece, down_ref[...], preferred_element_type=jnp.float32)
+    product = jnp.dot(
+        jnp.concatenate([low, middle, high], axis=0),
+        down_ref[...],
+        preferred_element_type=jnp.float32,
+    )
+    local_part = sum(product[i * n * tiles : (i + 1) * n * tiles] for i in range(3))
     here = z * heads + hd
     parts[here] = local_part.astype(jnp.bfloat16)
-    for k in range(n):
-        for j in range(heads):
+    for k in reversed(range(n)):
+        for j in reversed(range(heads)):
             if k or j:
                 send(
                     parts.at[here],
                     parts.at[here],
                     send_part.at[0],
                     recv_part.at[0],
-                    {"seq": seq_peer(k), "head": head_peer(j)},
+                    {"seq": ahead(k), "head": head_peer(j)},
                 )
     for buffer, receives in ((wcol_out, recv_aux.at[0]), (sub_out, recv_aux.at[1])):
         slot = buffer.at[pl.ds(0, heads - 1)]
@@ -997,8 +1021,9 @@
         betas.append((weights * inverse).reshape(head_count * new_count, step))
         alphas.append(old * inverse)
 
-    peers(new_mix, recv_kv.at[1])
-    inside_limit = jnp.where(query_at < limit, here_fresh.astype(jnp.float32), 0.0)
+    inside_limit = jnp.where(query_at < limit, here_fresh.astype(jnp.float32), 0.0).astype(
+        jnp.bfloat16
+    )
 
     def contract(left, right):
         return lax.dot_general(
@@ -1007,8 +1032,6 @@
 
     pieces = []
     for j in range(heads):
-        left = jnp.concatenate([by_head(new_kv[j, 1]), new_mix[j]], axis=0)
-        right = jnp.concatenate([betas[j], inside_limit], axis=0).astype(jnp.bfloat16)
         share_of = jnp.concatenate(
             [
                 mix_old[j, h * HEAD_DIM : (h + 1) * HEAD_DIM, :].astype(jnp.float32)
@@ -1017,11 +1040,13 @@
             ],
             axis=0,
         )
-        pieces.append(share_of + contract(left, right))
+        pieces.append(share_of + contract(by_head(new_kv[j, 1]), betas[j].astype(jnp.bfloat16)))
+    branch = sequence[z, hd].astype(jnp.float32) + contract(new_out[hd], here_fresh)
+    peers(new_mix, recv_kv.at[1])
+    pieces = [piece + contract(new_mix[j], inside_limit) for j, piece in enumerate(pieces)]
     mean = sum(jnp.sum(p, axis=0, keepdims=True) for p in pieces) / features
     square = sum(jnp.sum(p * p, axis=0, keepdims=True) for p in pieces) / features
     scaling = lax.rsqrt(square - mean * mean + layer_eps)
-    branch = sequence[z, hd].astype(jnp.float32) + contract(new_out[hd], here_fresh)
     for j in range(heads):
         gain = sub_col[pl.ds(j * cols, cols), :]
         settled = ((pieces[j] - mean) * scaling * gain).astype(jnp.bfloat16)
@@ -1042,8 +1067,7 @@
     drain(pre_out.at[pl.ds(0, 3)], send_fan.at[0])
     drain(wcol_out.at[pl.ds(0, heads - 1)], send_aux.at[0])
     drain(sub_out.at[pl.ds(0, heads - 1)], send_aux.at[1])
-    for c in range(blocks_c):
-        drain(pooled.at[pl.ds(0, 2 * n - 1), c], send_pool.at[c])
+    drain(pooled.at[pl.ds(0, 2 * n - 1)], send_pool.at[0])
     drain(means.at[pl.ds(0, n - 1)], send_mean.at[0])
     drain(parts.at[pl.ds(0, n * heads - 1)], send_part.at[0])
     drain(own_embed, send_new.at[0])
@@ -1131,23 +1155,25 @@
             pltpu.VMEM((blocks_k, blocks_c, 2, n * LANES, LANES), bf16),
             pltpu.VMEM((4, rows, blocks_c * 2 * LANES), f32),
             pltpu.VMEM((2, blocks_c, 2 * tiles, LANES), f32),
-            pltpu.VMEM((2 * n, blocks_c, 2 * tiles, LANES), f32),
+            pltpu.VMEM((2, 2 * tiles, blocks_c * LANES), f32),
+            pltpu.VMEM((2 * n, 2 * tiles, blocks_c * LANES), f32),
             pltpu.VMEM((heads, 1, width), f32),
             pltpu.VMEM((n, tiles, width), f32),
             pltpu.VMEM((n * heads, n * tiles, w_down.shape[1]), bf16),
             dma((17,)),
             dma((1,)),
-            dma((12, 2)),
+            dma((6, 2)),
+            dma((2,)),
             dma((1,)),
             dma((blocks_k * blocks_c,)),
             dma((2,)),
             dma((n,)),
             dma((1,)),
-            dma((3, n)),
+            dma((n,)),
             dma((2,)),
             dma((2,)),
-            dma((blocks_c,)),
-            dma((blocks_c,)),
+            dma((1,)),
+            dma((1,)),
             dma((1,)),
             dma((1,)),
             dma((1,)),

time: 68.8 us -> 67.9 us (0.987)
  Pallas kernels: 67.3 us -> 66.4 us
    pallas_call x1, Pallas kernels: 67.3 us -> 66.4 us  [near_body(): pl.pallas_call(functools.partial(encode_kernel, tiles), out_shape=pltpu.V...]
where the time goes in v4:
time: 67.9 us; the launch traced here: 67.7 us
  Pallas kernels  66.4 us (98%)
  local copies, waits for them, and re-layouts  0.68 us (1%)
    pallas_call x1, Pallas kernels, near_body(): pl.pallas_call(functools.partial(encode_kernel, tiles), out_shape=pltpu.V...  66.4 us

profile of v4, /device:TPU:0, one launch (start us, length us, event | category | flops | bytes accessed | tf_op | source)
XLA Modules:
  0.0 67.7 jit_solution(3668986288265014642)
XLA Ops:
  0.7 66.4 %shard_map.145 = f32[192,256]{1,0:T(8,128)S(1)} custom-call(s32[1]{0:T(128)S(6)} %copy.18.valid_ref, bf16[512,1536]{1,0:T(8,128)(2,1)} %bitcast.7, f32[1536]{0:T(1024)} %gain_hbm.1, f32[1536]{0:T(1024)} %scale_hbm.1, f32[1536]{0:T(1024)} %fc_hbm.1, bf16[2,384,1024]{2,1,0:T(8,128)(2,1)} %w_hbm.1, bf16[1024,384]{1,0:T(8,128)(2,1)} %down_hbm.1, ...), custom_call_target="tpu_custom_call" | custom-call | tf_op jit(solution)/shard_map/pallas_call | solution.py:1114
  67.0 0.7 %copy.17 = f32[256,192]{0,1:T(8,128)} copy(f32[256,192]{0,1:T(8,128)S(1)} %bitcast.6) | data formatting | bytes 393216

commit v5 on v4

--- a/solution.py
+++ b/solution.py
@@ -286,6 +286,8 @@
     down_ref,
     embed_ref,
     qkv_ref,
+    qkv_cols,
+    embed_cols,
     wcol_parts,
     narrow_ref,
     pre_own,
@@ -296,6 +298,8 @@
     sequence,
     queries,
     key_rows,
+    key_cols,
+    value_rows,
     value_cols,
     fresh,
     keep_rows,
@@ -310,7 +314,6 @@
     normed,
     wall,
     acc,
-    pool_parts,
     pool_mine,
     pooled,
     sums,
@@ -623,6 +626,9 @@
         )
         return jnp.sum(jnp.where(same, row, 0.0), axis=1, keepdims=True)
 
+    loads[0].wait()
+    for g in range(3):
+        qkv_cols[g] = qkv_ref[g].T
     features = heads * cols
     for start in range(0, features, LANES):
         at = pl.ds(start, LANES)
@@ -731,7 +737,9 @@
         ).astype(jnp.bfloat16)
         queries[t] = result[:cols]
         key_rows[at, :] = result[cols : 2 * cols].T
+        key_cols[:, t * step : (t + 1) * step] = result[cols : 2 * cols]
         value_cols[:, t * step : (t + 1) * step] = result[2 * cols :]
+        value_rows[at, :] = result[2 * cols :].T
 
     def attend_stored():
         query = queries[z]
@@ -767,7 +775,6 @@
                     {"head": head_peer(k)},
                 )
 
-    loads[0].wait()
     slot = pre_out.at[:, pl.ds(0, 2)]
     remote(slot, slot, send_fan.at[0], recv_mate.at[1], {"head": mate}).wait_recv()
     for t in range(n):
@@ -825,8 +832,7 @@
             arrived(r * blocks_c + c)
         w = gathered(r, range(blocks_c))
 
-        @pl.loop(0, 4)
-        def _(s):
+        for s in range(4):
             value = jnp.dot(token_block(s, r), w, preferred_element_type=jnp.float32)
             if r == 0:
                 acc[s] = value
@@ -838,29 +844,26 @@
         for c in range(blocks_c):
             arrived(r * blocks_c + c)
         w = gathered(r, range(blocks_c))
-
-        @pl.loop(0, 4)
-        def _(s):
-            value = acc[s] + jnp.dot(token_block(s, r), w, preferred_element_type=jnp.float32)
-            for c in range(blocks_c):
-                gate = value[:, 2 * c * LANES : (2 * c + 1) * LANES]
-                raised = value[:, (2 * c + 1) * LANES : (2 * c + 2) * LANES]
-                hidden = (gate / (1.0 + jnp.exp(-gate)) * raised).astype(jnp.bfloat16)
-                hidden = hidden.astype(jnp.float32)
-                for tile in range(tiles):
-                    pool_parts[s // 2, c, pl.ds(s % 2 * tiles + tile, 1), :] = (
-                        jnp.sum(hidden[tile * patch : (tile + 1) * patch], axis=0, keepdims=True)
-                        / patch
-                    )
-
-        for yy in range(2):
-            pool_mine[yy] = jnp.concatenate([pool_parts[yy, c] for c in range(blocks_c)], axis=1)
         place = y * n + z
-        pooled[place] = pool_mine[y]
-        for k in reversed(range(n)):
-            for other in range(2):
+        for other in (1, 0):
+            yy = 1 - y if other else y
+            for m in range(2):
+                s = yy * 2 + m
+                value = acc[s] + jnp.dot(token_block(s, r), w, preferred_element_type=jnp.float32)
+                for c in range(blocks_c):
+                    gate = value[:, 2 * c * LANES : (2 * c + 1) * LANES]
+                    raised = value[:, (2 * c + 1) * LANES : (2 * c + 2) * LANES]
+                    hidden = (gate / (1.0 + jnp.exp(-gate)) * raised).astype(jnp.bfloat16)
+                    hidden = hidden.astype(jnp.float32)
+                    for tile in range(tiles):
+                        pool_mine[
+                            yy, pl.ds(m * tiles + tile, 1), c * LANES : (c + 1) * LANES
+                        ] = (
+                            jnp.sum(hidden[tile * patch : (tile + 1) * patch], axis=0, keepdims=True)
+                            / patch
+                        )
+            for k in reversed(range(n)):
                 if k or other:
-                    yy = 1 - y if other else y
                     send(
                         pool_mine.at[yy],
                         pooled.at[place],
@@ -868,9 +871,16 @@
                         recv_pool.at[0],
                         {"groups": yy, "seq": ahead(k)},
                     )
+        pooled[place] = pool_mine[y]
 
     for r in range(blocks_k - 1):
         multiply(r)
+        if r == 0:
+            remote(own_embed, own_embed, send_new.at[0], recv_new.at[0], {"head": mate}).wait_recv()
+            for which, event in ((y, 3), (1 - y, 4)):
+                embed_copy(beyond, which, event, {"head": mate}).wait_recv()
+            for j in range(heads):
+                embed_cols[:, j * cols : (j + 1) * cols] = embed_ref[j].T
     pool()
 
     seen = means.at[pl.ds(0, n - 1)]
@@ -917,9 +927,6 @@
         sub_col[pl.ds(j * cols, cols), :] = column(sub_out[j, 1:2])
     slot = parts.at[pl.ds(0, n * heads - 1)]
     remote(slot, slot, send_part.at[0], recv_part.at[0], {"seq": partner}).wait_recv()
-    remote(own_embed, own_embed, send_new.at[0], recv_new.at[0], {"head": mate}).wait_recv()
-    for which, event in ((y, 3), (1 - y, 4)):
-        embed_copy(beyond, which, event, {"head": mate}).wait_recv()
     summed = jnp.concatenate(
         [
             sum(parts[b * heads + j].astype(jnp.float32) for j in range(heads))
@@ -931,9 +938,10 @@
     feature = normalize(
         average + scale_ref[...].reshape(1, width) * summed, fc_ref[...].reshape(1, width)
     ).astype(jnp.bfloat16)
-    table = embed_ref[...].reshape(heads * cols, width)
     shift = jnp.concatenate([sub_out[j, 0:1] for j in range(heads)], axis=1)
-    fresh_values = (dot_rows(feature, table) + shift).astype(jnp.bfloat16)
+    fresh_values = (
+        jnp.dot(feature, embed_cols[...], preferred_element_type=jnp.float32) + shift
+    ).astype(jnp.bfloat16)
     for j in range(heads):
         new_out[j] = fresh_values[:, j * cols : (j + 1) * cols]
     fresh_values = fresh_values.astype(jnp.float32)
@@ -944,7 +952,8 @@
 
     normal = normalize(fresh_values, slide_ref[...].reshape(1, features)).astype(jnp.bfloat16)
     new_query, new_key, new_value = [
-        dot_rows(normal, qkv_ref[g]).astype(jnp.bfloat16) for g in range(3)
+        jnp.dot(normal, qkv_cols[g], preferred_element_type=jnp.float32).astype(jnp.bfloat16)
+        for g in range(3)
     ]
     new_kv[hd, 0] = new_key
     new_kv[hd, 1] = new_value
@@ -969,7 +978,7 @@
     )[:, :new_count]
 
     many = by_head(new_query)
-    scores = dot_rows(many, key_rows[...]) * factor
+    scores = jnp.dot(many, key_cols[...], preferred_element_type=jnp.float32) * factor
     scores = jnp.where(keep_cols[...] > 0.0, scores, masked_score)
     recent = dot_rows(many, new_key) * factor
     recent = jnp.where(new_lane < limit, recent, masked_score)
@@ -984,7 +993,9 @@
     recent = jnp.exp(recent - peak) * multiplicity(new_lane, row_at, offset)
     mass = jnp.sum(weights, axis=1, keepdims=True) + jnp.sum(recent, axis=1, keepdims=True)
     attended = (
-        dot_rows(weights.astype(jnp.bfloat16), value_cols[...])
+        jnp.dot(
+            weights.astype(jnp.bfloat16), value_rows[...], preferred_element_type=jnp.float32
+        )
         + jnp.dot(recent.astype(jnp.bfloat16), new_value, preferred_element_type=jnp.float32)
     ) / mass
     new_mix[hd] = sum(
@@ -1130,6 +1141,8 @@
             pltpu.VMEM(w_down.shape, bf16),
             pltpu.VMEM((heads, cols, width), bf16),
             pltpu.VMEM((3, cols, heads * cols), bf16),
+            pltpu.VMEM((3, heads * cols, cols), bf16),
+            pltpu.VMEM((width, heads * cols), bf16),
             pltpu.VMEM((heads, cols, cols), bf16),
             pltpu.VMEM((2, cols), f32),
             pltpu.VMEM((cols, block_rows), bf16),
@@ -1139,6 +1152,8 @@
             pltpu.VMEM((heads, 2, cols), f32),
             pltpu.VMEM((n, heads, cols, block_rows), bf16),
             pltpu.VMEM((n, cols, block_rows), bf16),
+            pltpu.VMEM((total_rows, cols), bf16),
+            pltpu.VMEM((cols, total_rows), bf16),
             pltpu.VMEM((total_rows, cols), bf16),
             pltpu.VMEM((cols, total_rows), bf16),
             pltpu.VMEM((n, LANES, block_rows), bf16),
@@ -1154,7 +1169,6 @@
             pltpu.VMEM((4, heads, quarter, width), bf16),
             pltpu.VMEM((blocks_k, blocks_c, 2, n * LANES, LANES), bf16),
             pltpu.VMEM((4, rows, blocks_c * 2 * LANES), f32),
-            pltpu.VMEM((2, blocks_c, 2 * tiles, LANES), f32),
             pltpu.VMEM((2, 2 * tiles, blocks_c * LANES), f32),
             pltpu.VMEM((2 * n, 2 * tiles, blocks_c * LANES), f32),
             pltpu.VMEM((heads, 1, width), f32),

time: 67.9 us -> 65.3 us (0.962)
  Pallas kernels: 66.4 us -> 63.8 us
    pallas_call x1, Pallas kernels: 66.4 us -> 63.8 us  [near_body(): pl.pallas_call(functools.partial(encode_kernel, tiles), out_shape=pltpu.V...]
where the time goes in v5:
time: 65.3 us; the launch traced here: 65.2 us
  Pallas kernels  63.8 us (98%)
  local copies, waits for them, and re-layouts  0.68 us (1%)
  between operations  0.66 us (1%)
    pallas_call x1, Pallas kernels, near_body(): pl.pallas_call(functools.partial(encode_kernel, tiles), out_shape=pltpu.V...  63.8 us

profile of v5, /device:TPU:0, one launch (start us, length us, event | category | flops | bytes accessed | tf_op | source)
XLA Modules:
  0.0 65.2 jit_solution(4016649249305403152)
XLA Ops:
  0.7 63.8 %shard_map.145 = f32[192,256]{1,0:T(8,128)S(1)} custom-call(s32[1]{0:T(128)S(6)} %copy.18.valid_ref, bf16[512,1536]{1,0:T(8,128)(2,1)} %bitcast.7, f32[1536]{0:T(1024)} %gain_hbm.1, f32[1536]{0:T(1024)} %scale_hbm.1, f32[1536]{0:T(1024)} %fc_hbm.1, bf16[2,384,1024]{2,1,0:T(8,128)(2,1)} %w_hbm.1, bf16[1024,384]{1,0:T(8,128)(2,1)} %down_hbm.1, ...), custom_call_target="tpu_custom_call" | custom-call | tf_op jit(solution)/shard_map/pallas_call | solution.py:1125
  64.5 0.7 %copy.17 = f32[256,192]{0,1:T(8,128)} copy(f32[256,192]{0,1:T(8,128)S(1)} %bitcast.6) | data formatting | bytes 393216

commit v6 on v5

--- a/solution.py
+++ b/solution.py
@@ -318,6 +318,8 @@
     pooled,
     sums,
     means,
+    mean_in,
+    averages,
     parts,
     local_sem,
     send_tok,
@@ -605,11 +607,25 @@
     norm_quarter(3)
     for tile in range(tiles):
         per = heads // tiles
-        means[z, pl.ds(tile, 1), :] = (
-            sum(sums[tile * per + i] for i in range(per)) / patch
-        )
-    for k in range(1, n):
-        send(means.at[z], means.at[z], send_mean.at[0], recv_mean.at[0], {"seq": seq_peer(k)})
+        means[pl.ds(tile, 1), :] = sum(sums[tile * per + i] for i in range(per)) / patch
+    def mean_columns(owner):
+        return pl.ds(pl.multiple_of(owner * depth, LANES), depth)
+
+    averages[...] = jnp.zeros(averages.shape, jnp.float32)
+
+    @pl.when(hd == 0)
+    def _():
+        averages[z] = means[:, mean_columns(z)]
+        for k in range(1, n):
+            target = seq_peer(k)
+            send(
+                means.at[:, mean_columns(target)],
+                mean_in.at[z],
+                send_mean.at[0],
+                recv_mean.at[0],
+                {"seq": target},
+            )
+
     for load in small_loads[2:]:
         load.wait()
     narrow_ref[pl.ds(0, 1), :] = bias_ref[...].reshape(1, narrow)
@@ -883,8 +899,14 @@
                 embed_cols[:, j * cols : (j + 1) * cols] = embed_ref[j].T
     pool()
 
-    seen = means.at[pl.ds(0, n - 1)]
-    remote(seen, seen, send_mean.at[0], recv_mean.at[0], {"seq": partner}).wait_recv()
+
+    @pl.when(hd == 0)
+    def _():
+        seen = mean_in.at[pl.ds(0, n - 1)]
+        remote(seen, seen, send_mean.at[0], recv_mean.at[0], {"seq": partner}).wait_recv()
+        for k in range(1, n):
+            averages[seq_peer(k)] = mean_in[seq_peer(k)]
+
     slot = pooled.at[pl.ds(0, 2 * n - 1)]
     remote(slot, slot, send_pool.at[0], recv_pool.at[0], {"seq": partner}).wait_recv()
     loads[1].wait()
@@ -908,6 +930,9 @@
         preferred_element_type=jnp.float32,
     )
     local_part = sum(product[i * n * tiles : (i + 1) * n * tiles] for i in range(3))
+    local_part = local_part * scale_ref[mean_columns(z)].reshape(1, depth) + jnp.concatenate(
+        [averages[b] for b in range(n)], axis=0
+    )
     here = z * heads + hd
     parts[here] = local_part.astype(jnp.bfloat16)
     for k in reversed(range(n)):
@@ -934,10 +959,7 @@
         ],
         axis=1,
     )
-    average = jnp.concatenate([means[b] for b in range(n)], axis=0)
-    feature = normalize(
-        average + scale_ref[...].reshape(1, width) * summed, fc_ref[...].reshape(1, width)
-    ).astype(jnp.bfloat16)
+    feature = normalize(summed, fc_ref[...].reshape(1, width)).astype(jnp.bfloat16)
     shift = jnp.concatenate([sub_out[j, 0:1] for j in range(heads)], axis=1)
     fresh_values = (
         jnp.dot(feature, embed_cols[...], preferred_element_type=jnp.float32) + shift
@@ -1079,7 +1101,11 @@
     drain(wcol_out.at[pl.ds(0, heads - 1)], send_aux.at[0])
     drain(sub_out.at[pl.ds(0, heads - 1)], send_aux.at[1])
     drain(pooled.at[pl.ds(0, 2 * n - 1)], send_pool.at[0])
-    drain(means.at[pl.ds(0, n - 1)], send_mean.at[0])
+
+    @pl.when(hd == 0)
+    def _():
+        drain(mean_in.at[pl.ds(0, n - 1)], send_mean.at[0])
+
     drain(parts.at[pl.ds(0, n * heads - 1)], send_part.at[0])
     drain(own_embed, send_new.at[0])
     drain(embed_ref.at[pl.ds(0, 2)], send_new.at[1])
@@ -1172,7 +1198,9 @@
             pltpu.VMEM((2, 2 * tiles, blocks_c * LANES), f32),
             pltpu.VMEM((2 * n, 2 * tiles, blocks_c * LANES), f32),
             pltpu.VMEM((heads, 1, width), f32),
-            pltpu.VMEM((n, tiles, width), f32),
+            pltpu.VMEM((tiles, width), f32),
+            pltpu.VMEM((n, tiles, depth), f32),
+            pltpu.VMEM((n, tiles, depth), f32),
             pltpu.VMEM((n * heads, n * tiles, w_down.shape[1]), bf16),
             dma((17,)),
             dma((1,)),

time: 65.3 us -> 64.6 us (0.989)
  Pallas kernels: 63.8 us -> 63.1 us
    pallas_call x1, Pallas kernels: 63.8 us -> 63.1 us  [near_body(): pl.pallas_call(functools.partial(encode_kernel, tiles), out_shape=pltpu.V...]
where the time goes in v6:
time: 64.6 us; the launch traced here: 64.5 us
  Pallas kernels  63.1 us (98%)
  local copies, waits for them, and re-layouts  0.68 us (1%)
  between operations  0.66 us (1%)
    pallas_call x1, Pallas kernels, near_body(): pl.pallas_call(functools.partial(encode_kernel, tiles), out_shape=pltpu.V...  63.1 us

profile of v6, /device:TPU:0, one launch (start us, length us, event | category | flops | bytes accessed | tf_op | source)
XLA Modules:
  0.0 64.5 jit_solution(2939355358505131637)
XLA Ops:
  0.7 63.1 %shard_map.145 = f32[192,256]{1,0:T(8,128)S(1)} custom-call(s32[1]{0:T(128)S(6)} %copy.18.valid_ref, bf16[512,1536]{1,0:T(8,128)(2,1)} %bitcast.7, f32[1536]{0:T(1024)} %gain_hbm.1, f32[1536]{0:T(1024)} %scale_hbm.1, f32[1536]{0:T(1024)} %fc_hbm.1, bf16[2,384,1024]{2,1,0:T(8,128)(2,1)} %w_hbm.1, bf16[1024,384]{1,0:T(8,128)(2,1)} %down_hbm.1, ...), custom_call_target="tpu_custom_call" | custom-call | tf_op jit(solution)/shard_map/pallas_call | solution.py:1151
  63.8 0.7 %copy.17 = f32[256,192]{0,1:T(8,128)} copy(f32[256,192]{0,1:T(8,128)S(1)} %bitcast.6) | data formatting | bytes 393216

commit v7 on v6

--- a/solution.py
+++ b/solution.py
@@ -973,14 +973,16 @@
         remote(slot, slot, send_aux.at[0], receives, {"head": mate}).wait_recv()
 
     normal = normalize(fresh_values, slide_ref[...].reshape(1, features)).astype(jnp.bfloat16)
-    new_query, new_key, new_value = [
-        jnp.dot(normal, qkv_cols[g], preferred_element_type=jnp.float32).astype(jnp.bfloat16)
-        for g in range(3)
-    ]
+
+    def project_new(g):
+        return jnp.dot(normal, qkv_cols[g], preferred_element_type=jnp.float32).astype(jnp.bfloat16)
+
+    new_key, new_value = project_new(1), project_new(2)
     new_kv[hd, 0] = new_key
     new_kv[hd, 1] = new_value
     for k in range(1, heads):
         send(new_kv.at[hd], new_kv.at[hd], send_kv.at[0], recv_kv.at[0], {"head": head_peer(k)})
+    new_query = project_new(0)
     lane_head = lax.broadcasted_iota(jnp.int32, (1, cols), 1) // HEAD_DIM
     nothing = jnp.zeros((), jnp.bfloat16)
 

time: 64.6 us -> 64.8 us (level)
  no operation moved by 1% of the time
where the time goes in v7:
time: 64.8 us; the launch traced here: 64.7 us
  Pallas kernels  63.3 us (98%)
  local copies, waits for them, and re-layouts  0.68 us (1%)
  between operations  0.66 us (1%)
    pallas_call x1, Pallas kernels, near_body(): pl.pallas_call(functools.partial(encode_kernel, tiles), out_shape=pltpu.V...  63.3 us

profile of v7, /device:TPU:0, one launch (start us, length us, event | category | flops | bytes accessed | tf_op | source)
XLA Modules:
  0.0 64.7 jit_solution(14087042389404672548)
XLA Ops:
  0.7 63.3 %shard_map.145 = f32[192,256]{1,0:T(8,128)S(1)} custom-call(s32[1]{0:T(128)S(6)} %copy.18.valid_ref, bf16[512,1536]{1,0:T(8,128)(2,1)} %bitcast.7, f32[1536]{0:T(1024)} %gain_hbm.1, f32[1536]{0:T(1024)} %scale_hbm.1, f32[1536]{0:T(1024)} %fc_hbm.1, bf16[2,384,1024]{2,1,0:T(8,128)(2,1)} %w_hbm.1, bf16[1024,384]{1,0:T(8,128)(2,1)} %down_hbm.1, ...), custom_call_target="tpu_custom_call" | custom-call | tf_op jit(solution)/shard_map/pallas_call | solution.py:1153
  64.0 0.7 %copy.17 = f32[256,192]{0,1:T(8,128)} copy(f32[256,192]{0,1:T(8,128)S(1)} %bitcast.6) | data formatting | bytes 393216
